TPU v7x, 16 devices: a 4x2x1 block of a 4x4x8 slice. The times are simulated.
16 devices in a mesh: dp: 2 (over y, z), ep: 8 (over x, core).
Axes of the slice: x: 4, y: 2, z: 1, core: 2. Of those that a mesh axis runs over, the one named last changes fastest.
The devices are a block of a 4x4x8 slice.
Arguments:
- x_a: bfloat16 [2048, 2560], P(('dp', 'ep')), parts along dimension 0
- route_a: int32 [2048, 6], P(('dp', 'ep')), parts along dimension 0
- gate_a: float32 [2048, 6], P(('dp', 'ep')), parts along dimension 0
- h_b: bfloat16 [2048, 2560], P(('dp', 'ep')), parts along dimension 0
- attn_b: bfloat16 [2048, 2560], P(('dp', 'ep')), parts along dimension 0
- route_b: int32 [2048, 6], P(('dp', 'ep')), parts along dimension 0
- gate_b: float32 [2048, 6], P(('dp', 'ep')), parts along dimension 0
- w_qkv: bfloat16 [2560, 3584], replicated
- w_o: bfloat16 [2560, 2560], replicated
- w_gate: bfloat16 [64, 2560, 1536], P('ep')
- w_up: bfloat16 [64, 2560, 1536], P('ep')
- w_down: bfloat16 [64, 1536, 2560], P('ep')
Outputs:
- output 1: bfloat16 [2048, 2560], P(('dp', 'ep')), parts along dimension 0
- output 2: bfloat16 [2048, 2560], P(('dp', 'ep')), parts along dimension 0
- output 3: bfloat16 [2048, 3584], P(('dp', 'ep')), parts along dimension 0
There are 2 independent parts. A program takes and returns all parts, laid end to end along the dimension named above; an argument that names none is the same for every part.
All inputs are finite; a program needn't handle non-finite values.
Results may differ from a plain program's by a relative error of at most 0.0110739.
Values are sent between devices in bfloat16 or wider.
A program may use at most 768 MiB of HBM per device.

v0:
```python
import jax
import jax.numpy as jnp
from jax import lax
from jax.sharding import PartitionSpec as P


def route_slots(route_ids, n_experts, n_devs, capacity):
    tok_n, top_k = route_ids.shape
    local_n = n_experts // n_devs
    flat_route = route_ids.reshape(tok_n * top_k)
    one_hot = (flat_route[:, None] == jnp.arange(n_experts)[None, :]).astype(jnp.int32)
    slot_rank = jnp.sum((jnp.cumsum(one_hot, axis=0) - 1) * one_hot, axis=1)
    owner = flat_route // local_n
    local_id = flat_route % local_n
    slot_ids = local_id * (n_devs * capacity) + owner * capacity + slot_rank
    return slot_ids.reshape(tok_n, top_k)


def expert_ffn(rows_in, w_gate, w_up, w_down):
    gate_act = jnp.einsum('erd,edf->erf', rows_in, w_gate, preferred_element_type=jnp.float32)
    up_act = jnp.einsum('erd,edf->erf', rows_in, w_up, preferred_element_type=jnp.float32)
    hidden = (jax.nn.silu(gate_act) * up_act).astype(jnp.bfloat16)
    return jnp.einsum('erf,efd->erd', hidden, w_down, preferred_element_type=jnp.float32).astype(jnp.bfloat16)


def moe_local(tokens, route_ids, gate_vals, w_gate, w_up, w_down, n_devs):
    tok_n, model_dim = tokens.shape
    top_k = route_ids.shape[1]
    local_n = w_gate.shape[0]
    n_experts = local_n * n_devs
    capacity = min(tok_n, 2 * ((tok_n * top_k + n_experts - 1) // n_experts))
    n_slots = n_experts * capacity
    slot_ids = route_slots(route_ids, n_experts, n_devs, capacity)
    picker = (slot_ids[:, :, None] == jnp.arange(n_slots)[None, None, :]).astype(jnp.bfloat16)
    placer = jnp.sum(picker, axis=1)
    send_buf = jnp.einsum('ts,td->sd', placer, tokens, preferred_element_type=jnp.float32).astype(jnp.bfloat16)
    send_buf = send_buf.reshape(local_n, n_devs, capacity, model_dim)
    recv_buf = lax.all_to_all(send_buf, 'ep', 1, 1, tiled=True)
    expert_out = expert_ffn(recv_buf.reshape(local_n, n_devs * capacity, model_dim), w_gate, w_up, w_down)
    back_buf = lax.all_to_all(expert_out.reshape(local_n, n_devs, capacity, model_dim), 'ep', 1, 1, tiled=True)
    picked = jnp.einsum('tjs,sd->tjd', picker, back_buf.reshape(n_slots, model_dim), preferred_element_type=jnp.float32)
    mixture = jnp.zeros((tok_n, model_dim), jnp.float32)
    for choice in range(top_k):
        mixture = mixture + gate_vals[:, choice:choice + 1] * picked[:, choice]
    return (tokens.astype(jnp.float32) + mixture).astype(jnp.bfloat16)


def solution(mesh):
    n_devs = mesh.shape['ep']

    def local_step(x_a, route_a, gate_a, h_b, attn_b, route_b, gate_b, w_qkv, w_o, w_gate, w_up, w_down):
        out_a = moe_local(x_a, route_a, gate_a, w_gate, w_up, w_down, n_devs)
        qkv_b = jnp.dot(h_b, w_qkv, preferred_element_type=jnp.float32).astype(jnp.bfloat16)
        proj_b = jnp.dot(attn_b, w_o, preferred_element_type=jnp.float32).astype(jnp.bfloat16)
        mid_b = (h_b.astype(jnp.float32) + proj_b.astype(jnp.float32)).astype(jnp.bfloat16)
        out_b = moe_local(mid_b, route_b, gate_b, w_gate, w_up, w_down, n_devs)
        return out_a, out_b, qkv_b

    row_spec = P(('dp', 'ep'), None)
    full_spec = P(None, None)
    expert_spec = P('ep', None, None)
    return jax.shard_map(
        local_step,
        mesh=mesh,
        in_specs=(row_spec, row_spec, row_spec, row_spec, row_spec, row_spec, row_spec, full_spec, full_spec, expert_spec, expert_spec, expert_spec),
        out_specs=(row_spec, row_spec, row_spec),
        check_vma=False,
    )
```

profile of v0, /device:TPU:113, one launch (start us, length us, event | category | flops | bytes accessed | tf_op | source)
XLA Modules:
  0.0 434.3 jit_solution(4897528142224040205)
XLA Ops:
  0.6 0.9 copy.63
  1.8 1.8 reduce-window.16
  4.3 0.7 fusion.51
  5.6 0.7 fusion.10
  6.3 6.7 %fusion.8 = bf16[128,2560]{1,0:T(8,128)(2,1)S(1)} fusion(bf16[128,2560]{1,0:T(8,128)(2,1)S(1)} %copy-done, bf16[2560,2560]{1,0:T(8,128)(2,1)} %param.20, bf16[128,2560]{1,0:T(8,128)(2,1)} %param.15), kind=kOutput, calls=%fused_computation.18 | convolution fusion | flops 1679360000 | bytes 15073280 | tf_op jit(solution)/shard_map/dot_general | solution.py:54
  13.0 0.8 copy-done.2
  13.8 2.2 convolution_convert_fusion
  16.1 3.8 copy.67
  19.8 6.1 %all-to-all-start.2 = ((bf16[8,8,24,2560]{3,2,0,1:T(8,128)(2,1)}), bf16[8,8,24,2560]{3,2,0,1:T(8,128)(2,1)}, u32[]{:S(2)}, u32[]{:S(2)}) async-start(bf16[8,8,24,2560]{3,2,0,1:T(8,128)(2,1)} %copy.67), calls=%async_computation.2 | async-start | bytes 15728640 | tf_op jit(solution)/shard_map/all_to_all | solution.py:38
  26.4 1.8 reduce-window.14
  30.2 2.2 convolution_convert_fusion.1
  32.4 3.8 copy.59
  36.2 77.6 %all-to-all-done.2 = bf16[8,8,24,2560]{3,2,0,1:T(8,128)(2,1)} async-done(((bf16[8,8,24,2560]{3,2,0,1:T(8,128)(2,1)}), bf16[8,8,24,2560]{3,2,0,1:T(8,128)(2,1)}, u32[]{:S(2)}, u32[]{:S(2)}) %all-to-all-start.2) | async-done | bytes 7864352 | tf_op jit(solution)/shard_map/all_to_all | solution.py:38
  113.8 6.2 %all-to-all-start = ((bf16[8,8,24,2560]{3,2,0,1:T(8,128)(2,1)}), bf16[8,8,24,2560]{3,2,0,1:T(8,128)(2,1)}, u32[]{:S(2)}, u32[]{:S(2)}) async-start(bf16[8,8,24,2560]{3,2,0,1:T(8,128)(2,1)} %copy.59), calls=%async_computation | async-start | bytes 15728640 | tf_op jit(solution)/shard_map/all_to_all | solution.py:38
  120.0 7.1 %copy.68 = bf16[8,8,24,2560]{3,2,1,0:T(8,128)(2,1)} copy(bf16[8,8,24,2560]{3,2,0,1:T(8,128)(2,1)} %all-to-all-done.2) | data formatting | bytes 15728640 | tf_op jit(solution)/shard_map/all_to_all | solution.py:38
  127.1 29.9 %fusion.64 = f32[8,192,1536]{2,1,0:T(8,128)} fusion(bf16[8,192,2560]{2,1,0:T(8,128)(2,1)} %bitcast.189, bf16[8,2560,1536]{2,1,0:T(8,128)(2,1)} %param.21), kind=kOutput, calls=%fused_computation.120 | convolution fusion | flops 12079595520 | bytes 80216064 | tf_op jit(solution)/shard_map/erd,edf->erf/dot_general | solution.py:20
  157.0 53.6 %convolution_convert_fusion.2 = bf16[8,192,2560]{2,1,0:T(8,128)(2,1)} fusion(bf16[8,1536,2560]{2,1,0:T(8,128)(2,1)} %param.23, f32[8,192,1536]{2,1,0:T(8,128)} %fusion.64, bf16[8,192,2560]{2,1,0:T(8,128)(2,1)} %bitcast.190, bf16[8,2560,1536]{2,1,0:T(8,128)(2,1)} %param.22), kind=kOutput, calls=%fused_computation.4 | convolution fusion | flops 24177278976 | bytes 150994944 | tf_op jit(solution)/shard_map/erf,efd->erd/dot_general | solution.py:23
  210.7 7.1 %copy.69 = bf16[8,8,24,2560]{3,2,0,1:T(8,128)(2,1)} copy(bf16[8,8,24,2560]{3,2,1,0:T(8,128)(2,1)} %bitcast.197) | data formatting | bytes 15728640 | tf_op jit(solution)/shard_map/reshape | solution.py:40
  217.7 5.4 %all-to-all-start.3 = ((bf16[8,8,24,2560]{3,2,0,1:T(8,128)(2,1)}), bf16[8,8,24,2560]{3,2,0,1:T(8,128)(2,1)}, u32[]{:S(2)}, u32[]{:S(2)}) async-start(bf16[8,8,24,2560]{3,2,0,1:T(8,128)(2,1)} %copy.69), calls=%async_computation.3 | async-start | bytes 15728640 | tf_op jit(solution)/shard_map/all_to_all | solution.py:40
  223.1 7.1 %copy.60 = bf16[8,8,24,2560]{3,2,1,0:T(8,128)(2,1)} copy(bf16[8,8,24,2560]{3,2,0,1:T(8,128)(2,1)} %all-to-all-done) | data formatting | bytes 15728640 | tf_op jit(solution)/shard_map/all_to_all | solution.py:38
  230.2 29.9 %fusion.63 = f32[8,192,1536]{2,1,0:T(8,128)} fusion(bf16[8,192,2560]{2,1,0:T(8,128)(2,1)} %bitcast.191, bf16[8,2560,1536]{2,1,0:T(8,128)(2,1)} %param.21), kind=kOutput, calls=%fused_computation.119 | convolution fusion | flops 12079595520 | bytes 80216064 | tf_op jit(solution)/shard_map/erd,edf->erf/dot_general | solution.py:20
  260.1 53.6 %convolution_convert_fusion.3 = bf16[8,192,2560]{2,1,0:T(8,128)(2,1)} fusion(bf16[8,1536,2560]{2,1,0:T(8,128)(2,1)} %param.23, f32[8,192,1536]{2,1,0:T(8,128)} %fusion.63, bf16[8,192,2560]{2,1,0:T(8,128)(2,1)} %bitcast.192, bf16[8,2560,1536]{2,1,0:T(8,128)(2,1)} %param.22), kind=kOutput, calls=%fused_computation.5 | convolution fusion | flops 24177278976 | bytes 150994944 | tf_op jit(solution)/shard_map/erf,efd->erd/dot_general | solution.py:23
  313.7 7.1 %copy.61 = bf16[8,8,24,2560]{3,2,0,1:T(8,128)(2,1)} copy(bf16[8,8,24,2560]{3,2,1,0:T(8,128)(2,1)} %bitcast.198) | data formatting | bytes 15728640 | tf_op jit(solution)/shard_map/reshape | solution.py:40
  320.8 5.6 %all-to-all-start.1 = ((bf16[8,8,24,2560]{3,2,0,1:T(8,128)(2,1)}), bf16[8,8,24,2560]{3,2,0,1:T(8,128)(2,1)}, u32[]{:S(2)}, u32[]{:S(2)}) async-start(bf16[8,8,24,2560]{3,2,0,1:T(8,128)(2,1)} %copy.61), calls=%async_computation.1 | async-start | bytes 15728640 | tf_op jit(solution)/shard_map/all_to_all | solution.py:40
  326.4 9.7 %convolution_convert_fusion.4 = bf16[128,3584]{1,0:T(8,128)(2,1)} fusion(bf16[128,2560]{1,0:T(8,128)(2,1)S(1)} %copy-done.4, bf16[2560,3584]{1,0:T(8,128)(2,1)} %param.19), kind=kOutput, calls=%fused_computation.6 | convolution fusion | flops 2349268992 | bytes 19922944 | tf_op jit(solution)/shard_map/dot_general | solution.py:53
  336.1 3.9 copy.70
  340.1 8.9 %fusion = f32[128,6,2560]{2,0,1:T(8,128)} fusion(bf16[1536,2560,1]{1,0,2:T(8,128)(2,1)S(1)} %bitcast.199, s32[128,6]{0,1:T(8,128)S(1)} %copy-done.8), kind=kOutput, calls=%fused_computation.8 | convolution fusion | flops 6040977408 | bytes 15731712 | tf_op jit(solution)/shard_map/tjs,sd->tjd/dot_general | solution.py:41
  349.0 65.3 %all-to-all-done.1 = bf16[8,8,24,2560]{3,2,0,1:T(8,128)(2,1)} async-done(((bf16[8,8,24,2560]{3,2,0,1:T(8,128)(2,1)}), bf16[8,8,24,2560]{3,2,0,1:T(8,128)(2,1)}, u32[]{:S(2)}, u32[]{:S(2)}) %all-to-all-start.1) | async-done | bytes 7864352 | tf_op jit(solution)/shard_map/all_to_all | solution.py:40
  414.2 7.2 %copy.62 = bf16[8,8,24,2560]{3,2,1,0:T(8,128)(2,1)} copy(bf16[8,8,24,2560]{3,2,0,1:T(8,128)(2,1)} %all-to-all-done.1) | data formatting | bytes 15728640 | tf_op jit(solution)/shard_map/all_to_all | solution.py:40
  421.5 9.1 %fusion.4 = f32[128,6,2560]{2,0,1:T(8,128)S(1)} fusion(bf16[1536,2560,1]{1,0,2:T(8,128)(2,1)} %bitcast.200, s32[128,6]{0,1:T(8,128)S(1)} %copy-done.10), kind=kOutput, calls=%fused_computation.13 | convolution fusion | flops 6040977408 | bytes 15731712 | tf_op jit(solution)/shard_map/tjs,sd->tjd/dot_general | solution.py:41
  430.6 1.6 fusion.16
  432.2 1.6 fusion.29
  (55 shorter events, 3.9 us)
Async XLA Ops:
  0.6 5.7 %copy-start = (bf16[128,2560]{1,0:T(8,128)(2,1)S(1)}, bf16[128,2560]{1,0:T(8,128)(2,1)}, u32[]{:S(2)}) copy-start(bf16[128,2560]{1,0:T(8,128)(2,1)} %param.16) | copy-start | bytes 1966084
  5.0 0.6 copy-start.7
  13.0 0.8 copy-start.2
  19.8 6.1 %copy-start.11 = (s32[128,6]{0,1:T(8,128)S(1)}, s32[128,6]{0,1:T(8,128)}, u32[]{:S(2)}) copy-start(s32[128,6]{0,1:T(8,128)} %param.13) | copy-start | bytes 9220
  19.8 10.3 %copy-start.5 = (bf16[128,2560]{1,0:T(8,128)(2,1)S(1)}, bf16[128,2560]{1,0:T(8,128)(2,1)}, u32[]{:S(2)}) copy-start(bf16[128,2560]{1,0:T(8,128)(2,1)} %param.12) | copy-start | bytes 1966084
  19.8 94.0 %all-to-all-start.2 = ((bf16[8,8,24,2560]{3,2,0,1:T(8,128)(2,1)}), bf16[8,8,24,2560]{3,2,0,1:T(8,128)(2,1)}, u32[]{:S(2)}, u32[]{:S(2)}) async-start(bf16[8,8,24,2560]{3,2,0,1:T(8,128)(2,1)} %copy.67), calls=%async_computation.2 | async-start | bytes 15728640 | tf_op jit(solution)/shard_map/all_to_all | solution.py:38
  28.9 0.6 copy-start.9
  113.8 103.9 %all-to-all-start = ((bf16[8,8,24,2560]{3,2,0,1:T(8,128)(2,1)}), bf16[8,8,24,2560]{3,2,0,1:T(8,128)(2,1)}, u32[]{:S(2)}, u32[]{:S(2)}) async-start(bf16[8,8,24,2560]{3,2,0,1:T(8,128)(2,1)} %copy.59), calls=%async_computation | async-start | bytes 15728640 | tf_op jit(solution)/shard_map/all_to_all | solution.py:38
  217.7 103.1 %all-to-all-start.3 = ((bf16[8,8,24,2560]{3,2,0,1:T(8,128)(2,1)}), bf16[8,8,24,2560]{3,2,0,1:T(8,128)(2,1)}, u32[]{:S(2)}, u32[]{:S(2)}) async-start(bf16[8,8,24,2560]{3,2,0,1:T(8,128)(2,1)} %copy.69), calls=%async_computation.3 | async-start | bytes 15728640 | tf_op jit(solution)/shard_map/all_to_all | solution.py:40
  320.8 5.6 %copy-start.12 = (f32[128,6]{0,1:T(8,128)S(1)}, f32[128,6]{0,1:T(8,128)}, u32[]{:S(2)}) copy-start(f32[128,6]{0,1:T(8,128)} %param.18) | copy-start | bytes 9220
  320.8 5.6 %copy-start.13 = (f32[128,6]{0,1:T(8,128)S(1)}, f32[128,6]{0,1:T(8,128)}, u32[]{:S(2)}) copy-start(f32[128,6]{0,1:T(8,128)} %param.14) | copy-start | bytes 9220
  320.8 5.6 %copy-start.4 = (bf16[128,2560]{1,0:T(8,128)(2,1)S(1)}, bf16[128,2560]{1,0:T(8,128)(2,1)}, u32[]{:S(2)}) copy-start(bf16[128,2560]{1,0:T(8,128)(2,1)} %param.15) | copy-start | bytes 1966084
  320.8 93.4 %all-to-all-start.1 = ((bf16[8,8,24,2560]{3,2,0,1:T(8,128)(2,1)}), bf16[8,8,24,2560]{3,2,0,1:T(8,128)(2,1)}, u32[]{:S(2)}, u32[]{:S(2)}) async-start(bf16[8,8,24,2560]{3,2,0,1:T(8,128)(2,1)} %copy.61), calls=%async_computation.1 | async-start | bytes 15728640 | tf_op jit(solution)/shard_map/all_to_all | solution.py:40
  336.1 3.9 copy-start.8
  349.0 72.5 %copy-start.10 = (s32[128,6]{0,1:T(8,128)S(1)}, s32[128,6]{0,1:T(8,128)}, u32[]{:S(2)}) copy-start(s32[128,6]{0,1:T(8,128)} %copy-done.9) | copy-start | bytes 9220
  414.2 16.3 %slice-start = ((s8[7864320]{0:T(1024)(128)(4,1)}), s8[3670016]{0:T(1024)(128)(4,1)S(1)}, s32[]{:S(2)}) async-start(s8[7864320]{0:T(1024)(128)(4,1)} %bitcast.195), calls=%async_computation.4 | async-start | bytes 7340032
  421.5 9.1 %slice-start.1 = ((s8[7864320]{0:T(1024)(128)(4,1)}), s8[4194304]{0:T(1024)(128)(4,1)S(1)}, s32[]{:S(2)}) async-start(s8[7864320]{0:T(1024)(128)(4,1)} %bitcast.195), calls=%async_computation.5 | async-start | bytes 8388608
  421.5 9.1 %copy-start.3 = (bf16[128,2560]{1,0:T(8,128)(2,1)S(1)}, bf16[128,2560]{1,0:T(8,128)(2,1)}, u32[]{:S(2)}) copy-start(bf16[128,2560]{1,0:T(8,128)(2,1)} %copy-done.2) | copy-start | bytes 1966084
  430.6 1.7 copy-start.6
  430.6 3.3 copy-start.1
where the time goes:
time: 443 us; the launch traced here: 434 us
  matrix products  206 us (47%)
  waiting for transfers between devices  143 us (32%)
  local copies, waits for them, and re-layouts  51.5 us (12%)
  starting transfers between devices  23.3 us (5%)
  other arithmetic  9.32 us (2%)
    dot_general x2, matrix products, expert_ffn(): jnp.einsum('erf,efd->erd', hidden, w_down, preferred_element_type=jnp.flo...  107 us
    all_to_all x2, waiting for transfers between devices, moe_local(): recv_buf = lax.all_to_all(send_buf, 'ep', 1, 1, tiled=True)  77.7 us
    all_to_all x2, waiting for transfers between devices, moe_local(): lax.all_to_all(expert_out.reshape(local_n, n_devs, capacity, model_dim),...  65.3 us
    dot_general x2, matrix products, expert_ffn(): jnp.einsum('erd,edf->erf', rows_in, w_gate, preferred_element_type=jnp.fl...  59.8 us
    dot_general x2, matrix products, moe_local(): jnp.einsum('tjs,sd->tjd', picker, back_buf.reshape(n_slots, model_dim), p...  18 us
    all_to_all x2, local copies, waits for them, and re-layouts, moe_local(): recv_buf = lax.all_to_all(send_buf, 'ep', 1, 1, tiled=True)  14.2 us
    reshape x2, local copies, waits for them, and re-layouts, moe_local(): expert_out.reshape(local_n, n_devs, capacity, model_dim)  14.1 us
    all_to_all x2, starting transfers between devices, moe_local(): recv_buf = lax.all_to_all(send_buf, 'ep', 1, 1, tiled=True)  12.3 us
  transfers between devices with their start and end apart: 4, of which 2 were waited for; matrix products, arithmetic and copies ran while one was open for 52% of the time, Pallas kernels for 0%

commit v1 on v0

v1 whole, which is shorter than its diff:
```python
import functools

import jax
import jax.numpy as jnp
from jax import lax
from jax.experimental import pallas as pl
from jax.experimental.pallas import tpu as pltpu
from jax.sharding import PartitionSpec as P

F32 = jnp.float32
BF16 = jnp.bfloat16


def slot_map(routes, gates, first_expert, local_n, cap):
    n_src, tok_n, _ = routes.shape
    ids = first_expert + jnp.arange(local_n)
    hit = routes[:, None, :, :] == ids[None, :, None, None]
    member = jnp.any(hit, axis=3)
    gate = jnp.sum(jnp.where(hit, gates[:, None, :, :], 0.0), axis=3)
    tri = (jnp.arange(tok_n)[:, None] < jnp.arange(tok_n)[None, :]).astype(BF16)
    rank = jnp.einsum('sek,kt->set', member.astype(BF16), tri, preferred_element_type=F32).astype(jnp.int32)
    half = (jnp.arange(n_src) % 2)[:, None, None] * cap
    slot = jnp.where(member, rank + half, -1)

    def pair_up(a):
        return a.reshape(n_src // 2, 2, local_n, tok_n).transpose(0, 2, 1, 3).reshape(n_src // 2, local_n, 2 * tok_n)

    return pair_up(slot), pair_up(gate)


def pick(slot_row, n_slots):
    return lax.broadcasted_iota(jnp.int32, (n_slots, slot_row.shape[-1]), 0) == slot_row


def gate_up_kernel(cap2, x_ref, slot_ref, wg_ref, wu_ref, h_ref, rows):
    n_pair, local_n, width = slot_ref.shape

    @pl.when((pl.program_id(0) == 0) & (pl.program_id(1) == 0))
    def _():
        for p in range(n_pair):
            sel = jnp.concatenate([jnp.where(pick(slot_ref[p, e:e + 1, :], cap2), 1.0, 0.0) for e in range(local_n)], axis=0)
            got = jnp.dot(sel.astype(BF16), x_ref[p * width:(p + 1) * width, :], preferred_element_type=F32).astype(BF16)
            for e in range(local_n):
                rows[e, p * cap2:(p + 1) * cap2, :] = got[e * cap2:(e + 1) * cap2, :]

    mine = rows[pl.program_id(0)]
    gate = jnp.dot(mine, wg_ref[0], preferred_element_type=F32)
    up = jnp.dot(mine, wu_ref[0], preferred_element_type=F32)
    h_ref[0] = (jax.nn.silu(gate) * up).astype(BF16)


def gate_up(x_all, slot, w_gate, w_up, cap, fc=512):
    local_n, dim, ff = w_gate.shape
    n_pair = slot.shape[0]
    m = n_pair * 2 * cap
    return pl.pallas_call(
        functools.partial(gate_up_kernel, 2 * cap),
        out_shape=jax.ShapeDtypeStruct((local_n, m, ff), BF16),
        grid=(local_n, ff // fc),
        in_specs=[
            pl.BlockSpec(x_all.shape, lambda e, f: (0, 0)),
            pl.BlockSpec(slot.shape, lambda e, f: (0, 0, 0)),
            pl.BlockSpec((1, dim, fc), lambda e, f: (e, 0, f)),
            pl.BlockSpec((1, dim, fc), lambda e, f: (e, 0, f)),
        ],
        out_specs=pl.BlockSpec((1, m, fc), lambda e, f: (e, 0, f)),
        scratch_shapes=[pltpu.VMEM((local_n, m, dim), BF16)],
        compiler_params=pltpu.CompilerParams(vmem_limit_bytes=56 * 2 ** 20),
        cost_estimate=pl.CostEstimate(flops=4 * local_n * m * dim * ff, bytes_accessed=4 * local_n * dim * ff, transcendentals=0),
    )(x_all, slot, w_gate, w_up)


def down_kernel(cap2, slot_ref, gate_ref, h_ref, wd_ref, o_ref, ys):
    n_pair, local_n, width = slot_ref.shape
    e = pl.program_id(0)
    y = jnp.dot(h_ref[e], wd_ref[0], preferred_element_type=F32).astype(BF16)
    for p in range(n_pair):
        ys[p, pl.ds(pl.multiple_of(e * cap2, 16), cap2), :] = y[p * cap2:(p + 1) * cap2, :]

    @pl.when(e == local_n - 1)
    def _():
        for p in range(n_pair):
            parts = [[], [], []]
            for k in range(local_n):
                here = pick(slot_ref[p, k:k + 1, :], cap2)
                rest = gate_ref[p, k:k + 1, :]
                for part in parts:
                    head = rest.astype(BF16).astype(F32)
                    part.append(jnp.where(here, head, 0.0))
                    rest = rest - head
            total = None
            for part in parts:
                mat = jnp.concatenate(part, axis=0).astype(BF16)
                term = lax.dot_general(mat, ys[p], (((0,), (0,)), ((), ())), preferred_element_type=F32)
                total = term if total is None else total + term
            o_ref[p * width:(p + 1) * width, :] = total


def down(slot, gate, hidden, w_down, cap, start, cc):
    local_n, ff, dim = w_down.shape
    n_pair, _, width = slot.shape
    m = hidden.shape[1]
    return pl.pallas_call(
        functools.partial(down_kernel, 2 * cap),
        out_shape=jax.ShapeDtypeStruct((n_pair * width, cc), F32),
        grid=(local_n,),
        in_specs=[
            pl.BlockSpec(slot.shape, lambda e: (0, 0, 0)),
            pl.BlockSpec(gate.shape, lambda e: (0, 0, 0)),
            pl.BlockSpec(hidden.shape, lambda e: (0, 0, 0)),
            pl.BlockSpec((1, ff, cc), lambda e: (e, 0, start // cc)),
        ],
        out_specs=pl.BlockSpec((n_pair * width, cc), lambda e: (0, 0)),
        scratch_shapes=[pltpu.VMEM((n_pair, local_n * 2 * cap, cc), BF16)],
        compiler_params=pltpu.CompilerParams(vmem_limit_bytes=56 * 2 ** 20),
        cost_estimate=pl.CostEstimate(flops=2 * local_n * m * cc * ff, bytes_accessed=2 * local_n * cc * ff, transcendentals=0),
    )(slot, gate, hidden, w_down)


def solution(mesh):
    n_devs = mesh.shape['ep']

    def local_step(x_a, route_a, gate_a, h_b, attn_b, route_b, gate_b, w_qkv, w_o, w_gate, w_up, w_down):
        tok_n, dim = x_a.shape
        top_k = route_a.shape[1]
        local_n = w_gate.shape[0]
        n_experts = local_n * n_devs
        cap = min(tok_n, 2 * ((tok_n * top_k + n_experts - 1) // n_experts))
        cc = dim // 4
        small = jnp.concatenate([route_a.astype(F32), gate_a, route_b.astype(F32), gate_b], axis=1)
        small = lax.all_gather(small, 'ep')
        first = lax.axis_index('ep') * local_n
        slot_a, gw_a = slot_map(small[:, :, :top_k].astype(jnp.int32), small[:, :, top_k:2 * top_k], first, local_n, cap)
        slot_b, gw_b = slot_map(small[:, :, 2 * top_k:3 * top_k].astype(jnp.int32), small[:, :, 3 * top_k:], first, local_n, cap)

        all_a = lax.all_gather(x_a, 'ep', tiled=True)
        proj_b = jnp.dot(attn_b, w_o, preferred_element_type=F32).astype(BF16)
        mid_b = (h_b.astype(F32) + proj_b.astype(F32)).astype(BF16)
        all_b = lax.all_gather(mid_b, 'ep', tiled=True)

        def moe(tokens, everyone, slot, gw):
            hidden = gate_up(everyone, slot, w_gate, w_up, cap)
            outs = []
            for start in range(0, dim, cc):
                part = down(slot, gw, hidden, w_down, cap, start, cc)
                mix = lax.psum_scatter(part, 'ep', scatter_dimension=0, tiled=True)
                outs.append((tokens[:, start:start + cc].astype(F32) + mix).astype(BF16))
            return jnp.concatenate(outs, axis=1)

        out_a = moe(x_a, all_a, slot_a, gw_a)
        out_b = moe(mid_b, all_b, slot_b, gw_b)
        qkv_b = jnp.dot(h_b, w_qkv, preferred_element_type=F32).astype(BF16)
        return out_a, out_b, qkv_b

    row_spec = P(('dp', 'ep'), None)
    full_spec = P(None, None)
    expert_spec = P('ep', None, None)
    return jax.shard_map(
        local_step,
        mesh=mesh,
        in_specs=(row_spec, row_spec, row_spec, row_spec, row_spec, row_spec, row_spec, full_spec, full_spec, expert_spec, expert_spec, expert_spec),
        out_specs=(row_spec, row_spec, row_spec),
        check_vma=False,
    )
```

time: 443 us -> 385 us (0.87); the launches traced: 434 us -> 381 us
  Pallas kernels: 0 us -> 230 us
  matrix products: 206 us -> 18.8 us
  waiting for transfers between devices: 143 us -> 88 us
  local copies, waits for them, and re-layouts: 51.5 us -> 2.08 us
  starting transfers between devices: 23.3 us -> 1.3 us
  blocking collectives: 0 us -> 20.9 us
  between operations: 1.4 us -> 14.4 us
    pallas_call x0 -> x10, Pallas kernels: none -> 230 us  [the longest x8 123 us: down(): pl.pallas_call(functools.partial(down_kernel, 2 * cap), out_shape=jax.Sha...]
    dot_general x10 -> x4, matrix products: 206 us -> 18.8 us  [the longest x1 9.75 us: local_step(): qkv_b = jnp.dot(h_b, w_qkv, preferred_element_type=F32).astype(BF16)]
    all_to_all x4 -> x0, waiting for transfers between devices: 143 us -> none  [the longest x2 77.7 us: moe_local(): recv_buf = lax.all_to_all(send_buf, 'ep', 1, 1, tiled=True)]
    reduce_scatter x0 -> x8, waiting for transfers between devices: none -> 74.4 us  [moe(): mix = lax.psum_scatter(part, 'ep', scatter_dimension=0, tiled=True)]
    all_to_all x4 -> x0, local copies, waits for them, and re-layouts: 25.3 us -> none  [the longest x2 14.2 us: moe_local(): recv_buf = lax.all_to_all(send_buf, 'ep', 1, 1, tiled=True)]
    all_to_all x4 -> x0, starting transfers between devices: 23.3 us -> none  [the longest x2 12.3 us: moe_local(): recv_buf = lax.all_to_all(send_buf, 'ep', 1, 1, tiled=True)]
    reshape x4 -> x0, local copies, waits for them, and re-layouts: 21.7 us -> none  [the longest x2 14.1 us: moe_local(): expert_out.reshape(local_n, n_devs, capacity, model_dim)]
    all_gather x0 -> x1, blocking collectives: none -> 20.9 us  [local_step(): small = lax.all_gather(small, 'ep')]
  transfers between devices with their start and end apart: 4 -> 10, of which waited for: 2 -> 4; matrix products, arithmetic and copies ran while one was open for 52% -> 4% of each run, Pallas kernels for 0% -> 60%
where the time goes in v1:
time: 385 us; the launch traced here: 381 us
  Pallas kernels  230 us (60%)
  waiting for transfers between devices  88 us (23%)
  blocking collectives  20.9 us (5%)
  matrix products  18.8 us (5%)
  between operations  14.4 us (4%)
  other arithmetic  5.5 us (1%)
    pallas_call x8, Pallas kernels, down(): pl.pallas_call(functools.partial(down_kernel, 2 * cap), out_shape=jax.Sha...  123 us
    pallas_call x2, Pallas kernels, gate_up(): pl.pallas_call(functools.partial(gate_up_kernel, 2 * cap), out_shape=jax....  108 us
    reduce_scatter x8, waiting for transfers between devices, moe(): mix = lax.psum_scatter(part, 'ep', scatter_dimension=0, tiled=True)  74.4 us
    all_gather x1, blocking collectives, local_step(): small = lax.all_gather(small, 'ep')  20.9 us
    all_gather x1, waiting for transfers between devices, local_step(): all_b = lax.all_gather(mid_b, 'ep', tiled=True)  12.4 us
    dot_general x1, matrix products, local_step(): qkv_b = jnp.dot(h_b, w_qkv, preferred_element_type=F32).astype(BF16)  9.75 us
  transfers between devices with their start and end apart: 10, of which 4 were waited for; matrix products, arithmetic and copies ran while one was open for 4% of the time, Pallas kernels for 60%

profile of v1, /device:TPU:113, one launch (start us, length us, event | category | flops | bytes accessed | tf_op | source)
XLA Modules:
  0.0 381.2 jit_solution(13046068146378952327)
XLA Ops:
  7.3 1.0 copy-done
  8.3 7.5 %fusion.2 = bf16[128,2560]{1,0:T(8,128)(2,1)} fusion(bf16[128,2560]{1,0:T(8,128)(2,1)S(1)} %copy-done, bf16[2560,2560]{1,0:T(8,128)(2,1)} %param.20, bf16[128,2560]{1,0:T(8,128)(2,1)} %param.15), kind=kOutput, calls=%fused_computation.4 | convolution fusion | flops 1679360000 | bytes 15073280 | tf_op jit(solution)/shard_map/dot_general | solution.py:137
  15.9 0.7 all-gather.4.cloned.1.call-update
  16.8 20.9 %all-gather = f32[1024,24]{0,1:T(8,128)S(1)} all-gather(f32[128,24]{0,1:T(8,128)S(1)} %pad_maximum_fusion.2), channel_id=2, replica_groups=mesh['dp'=2,'ep'=8] {'ep'}, dimensions={0}, use_global_device_ids=true | all-gather | bytes 110592 | tf_op jit(solution)/shard_map/all_gather | solution.py:131
  37.8 0.1 compare_reduce_fusion
  38.0 0.7 fusion.8
  38.7 0.7 fusion.4
  39.4 12.4 %all-gather.6.cloned.1.call-done.x_ref = bf16[1024,2560]{1,0:T(8,128)(2,1)} async-done(((bf16[128,2560]{1,0:T(8,128)(2,1)}), bf16[1024,2560]{1,0:T(8,128)(2,1)}) %all-gather.6.cloned.1.call-update) | async-done | bytes 5242896 | tf_op jit(solution)/shard_map/all_gather | solution.py:139
  51.9 53.9 %shard_map.144.h_ref = bf16[8,192,1536]{2,1,0:T(8,128)(2,1)} custom-call(bf16[1024,2560]{1,0:T(8,128)(2,1)} %all-gather.6.cloned.1.call-done.x_ref, s32[4,8,256]{2,1,0:T(8,128)} %bitcast.39, bf16[8,2560,1536]{2,1,0:T(8,128)(2,1)} %wg_ref.3, bf16[8,2560,1536]{2,1,0:T(8,128)(2,1)} %wu_ref.3), custom_call_target="tpu_custom_call" | custom-call | flops 24159191040 | bytes 125829120 | tf_op jit(solution)/shard_map/pallas_call | solution.py:56
  105.8 15.3 %shard_map.145 = f32[1024,640]{1,0:T(8,128)} custom-call(s32[4,8,256]{2,1,0:T(8,128)} %bitcast.40, f32[4,8,256]{2,1,0:T(8,128)} %bitcast.48, bf16[8,192,1536]{2,1,0:T(8,128)(2,1)} %shard_map.144.h_ref, bf16[8,1536,2560]{2,1,0:T(8,128)(2,1)} %wd_ref.15), custom_call_target="tpu_custom_call" | custom-call | flops 3019898880 | bytes 15728640 | tf_op jit(solution)/shard_map/pallas_call | solution.py:103
  121.2 0.2 reduce-scatter.19.cloned.1.call-start
  121.4 15.3 %shard_map.146 = f32[1024,640]{1,0:T(8,128)} custom-call(s32[4,8,256]{2,1,0:T(8,128)} %bitcast.41, f32[4,8,256]{2,1,0:T(8,128)} %bitcast.49, bf16[8,192,1536]{2,1,0:T(8,128)(2,1)} %shard_map.144.h_ref, bf16[8,1536,2560]{2,1,0:T(8,128)(2,1)} %wd_ref.15), custom_call_target="tpu_custom_call" | custom-call | flops 3019898880 | bytes 15728640 | tf_op jit(solution)/shard_map/pallas_call | solution.py:103
  136.9 15.3 %shard_map.147 = f32[1024,640]{1,0:T(8,128)} custom-call(s32[4,8,256]{2,1,0:T(8,128)} %bitcast.42, f32[4,8,256]{2,1,0:T(8,128)} %bitcast.50, bf16[8,192,1536]{2,1,0:T(8,128)(2,1)} %shard_map.144.h_ref, bf16[8,1536,2560]{2,1,0:T(8,128)(2,1)} %wd_ref.15), custom_call_target="tpu_custom_call" | custom-call | flops 3019898880 | bytes 15728640 | tf_op jit(solution)/shard_map/pallas_call | solution.py:103
  152.3 15.4 %shard_map.148 = f32[1024,640]{1,0:T(8,128)} custom-call(s32[4,8,256]{2,1,0:T(8,128)} %bitcast.43, f32[4,8,256]{2,1,0:T(8,128)} %bitcast.51, bf16[8,192,1536]{2,1,0:T(8,128)(2,1)} %shard_map.144.h_ref, bf16[8,1536,2560]{2,1,0:T(8,128)(2,1)} %wd_ref.15), custom_call_target="tpu_custom_call" | custom-call | flops 3019898880 | bytes 15728640 | tf_op jit(solution)/shard_map/pallas_call | solution.py:103
  167.8 0.3 reduce-scatter.11.cloned.1.call-start
  168.1 0.8 fusion.6
  168.8 53.7 %shard_map.139.h_ref = bf16[8,192,1536]{2,1,0:T(8,128)(2,1)} custom-call(bf16[1024,2560]{1,0:T(8,128)(2,1)} %all-gather.4.cloned.1.call-done.x_ref, s32[4,8,256]{2,1,0:T(8,128)} %bitcast.34, bf16[8,2560,1536]{2,1,0:T(8,128)(2,1)} %wg_ref.3, bf16[8,2560,1536]{2,1,0:T(8,128)(2,1)} %wu_ref.3), custom_call_target="tpu_custom_call" | custom-call | flops 24159191040 | bytes 125829120 | tf_op jit(solution)/shard_map/pallas_call | solution.py:56
  222.6 15.3 %shard_map.141 = f32[1024,640]{1,0:T(8,128)} custom-call(s32[4,8,256]{2,1,0:T(8,128)} %bitcast.35, f32[4,8,256]{2,1,0:T(8,128)} %bitcast.44, bf16[8,192,1536]{2,1,0:T(8,128)(2,1)} %shard_map.139.h_ref, bf16[8,1536,2560]{2,1,0:T(8,128)(2,1)} %wd_ref.15), custom_call_target="tpu_custom_call" | custom-call | flops 3019898880 | bytes 15728640 | tf_op jit(solution)/shard_map/pallas_call | solution.py:103
  237.9 0.1 reduce-scatter.13.cloned.1.call-start
  238.0 15.3 %shard_map.142 = f32[1024,640]{1,0:T(8,128)} custom-call(s32[4,8,256]{2,1,0:T(8,128)} %bitcast.36, f32[4,8,256]{2,1,0:T(8,128)} %bitcast.45, bf16[8,192,1536]{2,1,0:T(8,128)(2,1)} %shard_map.139.h_ref, bf16[8,1536,2560]{2,1,0:T(8,128)(2,1)} %wd_ref.15), custom_call_target="tpu_custom_call" | custom-call | flops 3019898880 | bytes 15728640 | tf_op jit(solution)/shard_map/pallas_call | solution.py:103
  253.5 15.3 %shard_map.143 = f32[1024,640]{1,0:T(8,128)} custom-call(s32[4,8,256]{2,1,0:T(8,128)} %bitcast.37, f32[4,8,256]{2,1,0:T(8,128)} %bitcast.46, bf16[8,192,1536]{2,1,0:T(8,128)(2,1)} %shard_map.139.h_ref, bf16[8,1536,2560]{2,1,0:T(8,128)(2,1)} %wd_ref.15), custom_call_target="tpu_custom_call" | custom-call | flops 3019898880 | bytes 15728640 | tf_op jit(solution)/shard_map/pallas_call | solution.py:103
  268.8 0.3 reduce-scatter.9.cloned.1.call-start
  269.2 15.3 %shard_map.140 = f32[1024,640]{1,0:T(8,128)} custom-call(s32[4,8,256]{2,1,0:T(8,128)} %bitcast.38, f32[4,8,256]{2,1,0:T(8,128)} %bitcast.47, bf16[8,192,1536]{2,1,0:T(8,128)(2,1)} %shard_map.139.h_ref, bf16[8,1536,2560]{2,1,0:T(8,128)(2,1)} %wd_ref.15), custom_call_target="tpu_custom_call" | custom-call | flops 3019898880 | bytes 15728640 | tf_op jit(solution)/shard_map/pallas_call | solution.py:103
  284.5 1.0 copy-done.3
  285.6 9.8 %convolution_convert_fusion = bf16[128,3584]{1,0:T(8,128)(2,1)} fusion(bf16[128,2560]{1,0:T(8,128)(2,1)S(1)} %copy-done.3, bf16[2560,3584]{1,0:T(8,128)(2,1)} %param.19), kind=kOutput, calls=%fused_computation | convolution fusion | flops 2349268992 | bytes 19922944 | tf_op jit(solution)/shard_map/dot_general | solution.py:152
  295.4 1.4 add_convert_fusion.3
  296.8 0.9 pad_maximum_fusion.1
  297.7 10.6 %reduce-scatter.13.cloned.1.call-done = f32[128,640]{1,0:T(8,128)} async-done(((f32[1024,640]{1,0:T(8,128)}), f32[128,640]{1,0:T(8,128)}) %reduce-scatter.13.cloned.1.call-update) | async-done | bytes 327696 | tf_op jit(solution)/shard_map/reduce_scatter | solution.py:146
  308.3 32.0 %reduce-scatter.15.cloned.1.call-done = f32[128,640]{1,0:T(8,128)} async-done(((f32[1024,640]{1,0:T(8,128)}), f32[128,640]{1,0:T(8,128)}) %reduce-scatter.15.cloned.1.call-update) | async-done | bytes 327696 | tf_op jit(solution)/shard_map/reduce_scatter | solution.py:146
  340.3 31.8 %reduce-scatter.9.cloned.1.call-done = f32[128,640]{1,0:T(8,128)} async-done(((f32[1024,640]{1,0:T(8,128)}), f32[128,640]{1,0:T(8,128)}) %reduce-scatter.9.cloned.1.call-update) | async-done | bytes 327696 | tf_op jit(solution)/shard_map/reduce_scatter | solution.py:146
  372.1 1.4 add_convert_fusion.7
  373.4 0.9 pad_maximum_fusion
  (47 shorter events, 1.0 us)
Async XLA Ops:
  7.2 1.1 copy-start
  7.2 9.6 %copy-start.7 = (s32[128,6]{0,1:T(8,128)S(1)}, s32[128,6]{0,1:T(8,128)}, u32[]{:S(2)}) copy-start(s32[128,6]{0,1:T(8,128)} %param.13) | copy-start | bytes 9220
  7.2 9.6 %copy-start.8 = (s32[128,6]{0,1:T(8,128)S(1)}, s32[128,6]{0,1:T(8,128)}, u32[]{:S(2)}) copy-start(s32[128,6]{0,1:T(8,128)} %param.17) | copy-start | bytes 9220
  7.2 9.6 %copy-start.6 = (f32[128,6]{0,1:T(8,128)S(1)}, f32[128,6]{0,1:T(8,128)}, u32[]{:S(2)}) copy-start(f32[128,6]{0,1:T(8,128)} %param.14) | copy-start | bytes 9220
  7.2 9.6 %copy-start.5 = (f32[128,6]{0,1:T(8,128)S(1)}, f32[128,6]{0,1:T(8,128)}, u32[]{:S(2)}) copy-start(f32[128,6]{0,1:T(8,128)} %param.18) | copy-start | bytes 9220
  7.2 44.6 %all-gather.6.cloned.1.call-start = ((), (), s32[]{:S(2)}) async-start(), calls=%async_computation.13 | async-start | bytes 5898240 | tf_op jit(solution)/shard_map/all_gather | solution.py:139
  15.9 153.0 %all-gather.4.cloned.1.call-start = ((), (), s32[]{:S(2)}) async-start(), calls=%async_computation.8 | async-start | bytes 5898240 | tf_op jit(solution)/shard_map/all_gather | solution.py:136
  16.7 278.6 %reduce-scatter.17.cloned.1.call-start = ((), (), s32[]{:S(2)}) async-start(), calls=%async_computation.14 | async-start | bytes 2949120 | tf_op jit(solution)/shard_map/reduce_scatter | solution.py:146
  121.2 174.2 %reduce-scatter.19.cloned.1.call-start = ((), (), s32[]{:S(2)}) async-start(), calls=%async_computation.15 | async-start | bytes 2949120 | tf_op jit(solution)/shard_map/reduce_scatter | solution.py:146
  136.8 158.5 %reduce-scatter.21.cloned.1.call-start = ((), (), s32[]{:S(2)}) async-start(), calls=%async_computation.16 | async-start | bytes 2949120 | tf_op jit(solution)/shard_map/reduce_scatter | solution.py:146
  152.2 143.1 %reduce-scatter.23.cloned.1.call-start = ((), (), s32[]{:S(2)}) async-start(), calls=%async_computation.17 | async-start | bytes 2949120 | tf_op jit(solution)/shard_map/reduce_scatter | solution.py:146
  167.8 130.0 %reduce-scatter.11.cloned.1.call-start = ((), (), s32[]{:S(2)}) async-start(), calls=%async_computation.10 | async-start | bytes 2949120 | tf_op jit(solution)/shard_map/reduce_scatter | solution.py:146
  237.9 70.4 %reduce-scatter.13.cloned.1.call-start = ((), (), s32[]{:S(2)}) async-start(), calls=%async_computation.11 | async-start | bytes 2949120 | tf_op jit(solution)/shard_map/reduce_scatter | solution.py:146
  253.4 86.9 %reduce-scatter.15.cloned.1.call-start = ((), (), s32[]{:S(2)}) async-start(), calls=%async_computation.12 | async-start | bytes 2949120 | tf_op jit(solution)/shard_map/reduce_scatter | solution.py:146
  268.8 103.2 %reduce-scatter.9.cloned.1.call-start = ((), (), s32[]{:S(2)}) async-start(), calls=%async_computation.9 | async-start | bytes 2949120 | tf_op jit(solution)/shard_map/reduce_scatter | solution.py:146
  284.5 1.1 copy-start.3
  285.6 9.8 %copy-start.2 = (bf16[128,2560]{1,0:T(8,128)(2,1)S(1)}, bf16[128,2560]{1,0:T(8,128)(2,1)}, u32[]{:S(2)}) copy-start(bf16[128,2560]{1,0:T(8,128)(2,1)} %fusion.2) | copy-start | bytes 1966084
  295.3 76.7 %copy-start.4 = (bf16[128,2560]{1,0:T(8,128)(2,1)S(1)}, bf16[128,2560]{1,0:T(8,128)(2,1)}, u32[]{:S(2)}) copy-start(bf16[128,2560]{1,0:T(8,128)(2,1)} %param.12) | copy-start | bytes 1966084
  296.8 77.5 %copy-start.1 = (bf16[128,2560]{1,0:T(8,128)(2,1)S(1)}, bf16[128,2560]{1,0:T(8,128)(2,1)}, u32[]{:S(2)}) copy-start(bf16[128,2560]{1,0:T(8,128)(2,1)} %param.16) | copy-start | bytes 1966084
Sparse Core Ops, SparseCore 0:
  16.0 35.8 all-gather.5
  53.4 32.1 all-gather.3
  121.3 27.3 reduce-scatter.16
  150.9 29.6 reduce-scatter.18
  182.7 29.6 reduce-scatter.20
  214.6 29.6 reduce-scatter.22
  246.6 29.6 reduce-scatter.10
  278.6 29.6 reduce-scatter.12
  310.6 29.6 reduce-scatter.14
  342.4 29.6 reduce-scatter.8

commit v2 on v0

v2 whole, which is shorter than its diff:
```python
import functools

import jax
import jax.numpy as jnp
from jax import lax
from jax.experimental import pallas as pl
from jax.experimental.pallas import tpu as pltpu
from jax.sharding import PartitionSpec as P

F32 = jnp.float32
BF16 = jnp.bfloat16
RING = 8
WIDE = 512


def moe_kernel(n_devs, top_k, cap, x_ref, h_ref, attn_ref, meta_ref, wqkv_ref, wo_ref, wg_ref, wu_ref, wd_ref,
               outa_ref, outb_ref, qkv_ref,
               ring, xbuf, mbuf, ubuf, rows, hidden, slots, gts, ys, p0, p1, dr, ri, fl, fr,
               ring_sem, ag_send, ag_recv, me_send, me_recv, rs_send, rs_recv, x_free, rs_free):
    tok_n, dim = x_ref.shape
    half = tok_n // 2
    local_n, _, ff = wg_ref.shape
    qkv_n = wqkv_ref.shape[1]
    cap2 = 2 * cap
    n_pair = n_devs // 2
    n_slot = local_n * cap2
    me = lax.axis_index('ep')
    core = lax.rem(me, 2)
    partner = me + 1 - 2 * core
    right = lax.rem(me + 2, n_devs)
    left = lax.rem(me + n_devs - 2, n_devs)
    first = (me * local_n).astype(F32)
    peers = (partner, left, right)

    def signal_peers(sem):
        for peer in peers:
            pl.semaphore_signal(sem, inc=1, device_id={'ep': peer}, device_id_type=pl.DeviceIdType.MESH)

    n_o, n_f, n_q, n_w = dim // WIDE, ff // WIDE, dim // WIDE, qkv_n // WIDE
    n_gu, n_d = local_n * n_f, local_n * n_q
    at_ga = n_o
    at_da = at_ga + 2 * n_gu
    at_gb = at_da + n_d
    at_db = at_gb + 2 * n_gu
    at_w = at_db + n_d
    at_end = at_w + n_w

    def cols(k):
        return pl.ds(pl.multiple_of(k * WIDE, WIDE), WIDE)

    def tall_copy(src, idx):
        slot = lax.rem(idx, RING)
        return pltpu.make_async_copy(src, ring.at[slot], ring_sem.at[slot])

    def down_copy(e, k, idx):
        slot = lax.rem(idx, RING)
        return pltpu.make_async_copy(wd_ref.at[e, :, cols(k)], ring.at[slot, pl.ds(0, ff)], ring_sem.at[slot])

    def start_gu(t, idx):
        step = t // 2
        e, f = step // n_f, step % n_f

        @pl.when(t % 2 == 0)
        def _():
            tall_copy(wg_ref.at[e, :, cols(f)], idx).start()

        @pl.when(t % 2 == 1)
        def _():
            tall_copy(wu_ref.at[e, :, cols(f)], idx).start()

    def fetch(idx, kinds):
        if 'o' in kinds:
            @pl.when(idx < at_ga)
            def _():
                tall_copy(wo_ref.at[:, cols(idx)], idx).start()
        for name, base in (('ga', at_ga), ('gb', at_gb)):
            if name in kinds:
                @pl.when((idx >= base) & (idx < base + 2 * n_gu))
                def _():
                    start_gu(idx - base, idx)
        for name, base in (('da', at_da), ('db', at_db)):
            if name in kinds:
                @pl.when((idx >= base) & (idx < base + n_d))
                def _():
                    t = idx - base
                    down_copy(t % local_n, t // local_n, idx).start()
        if 'w' in kinds:
            @pl.when((idx >= at_w) & (idx < at_end))
            def _():
                tall_copy(wqkv_ref.at[:, cols(idx - at_w)], idx).start()

    def tall(idx):
        tall_copy(wo_ref.at[:, pl.ds(0, WIDE)], idx).wait()
        return ring[lax.rem(idx, RING)]

    lo, hi = pl.ds(0, half), pl.ds(half, half)

    def ag(m, k):
        own = x_ref if m == 0 else ubuf
        src, dst, to = (
            (own.at[lo], xbuf.at[1, 0, lo], right),
            (own.at[hi], xbuf.at[1, 0, hi], right),
            (own.at[hi], xbuf.at[2, 0, hi], left),
            (own.at[lo], xbuf.at[2, 0, lo], left),
            (own, xbuf.at[0, 1], partner),
            (xbuf.at[1, 0, lo], xbuf.at[3, 0, lo], right),
            (xbuf.at[2, 0, hi], xbuf.at[3, 0, hi], left),
            (xbuf.at[1, 0], xbuf.at[1, 1], partner),
            (xbuf.at[2, 0], xbuf.at[2, 1], partner),
            (xbuf.at[3, 0, lo], xbuf.at[3, 1, lo], partner),
            (xbuf.at[3, 0, hi], xbuf.at[3, 1, hi], partner),
        )[k]
        return pltpu.make_async_remote_copy(src_ref=src, dst_ref=dst, send_sem=ag_send.at[m, k], recv_sem=ag_recv.at[m, k],
                                            device_id={'ep': to}, device_id_type=pl.DeviceIdType.MESH)

    def meta(k):
        src, dst, to = (
            (meta_ref, mbuf.at[1, 0], right),
            (meta_ref, mbuf.at[2, 0], left),
            (meta_ref, mbuf.at[0, 1], partner),
            (mbuf.at[1, 0], mbuf.at[3, 0], right),
            (mbuf.at[1, 0], mbuf.at[1, 1], partner),
            (mbuf.at[2, 0], mbuf.at[2, 1], partner),
            (mbuf.at[3, 0], mbuf.at[3, 1], partner),
        )[k]
        return pltpu.make_async_remote_copy(src_ref=src, dst_ref=dst, send_sem=me_send.at[k], recv_sem=me_recv.at[k],
                                            device_id={'ep': to}, device_id_type=pl.DeviceIdType.MESH)

    def rs(k, q):
        src, dst, to = (
            (p1.at[lax.rem(q, 2)], dr.at[q], partner),
            (p0.at[q, 3, lo], ri.at[q, 0], right),
            (p0.at[q, 3, hi], ri.at[q, 1], left),
            (p0.at[q, 2, hi], fl.at[q, hi], right),
            (p0.at[q, 1, lo], fr.at[q, lo], left),
            (p0.at[q, 2, lo], fl.at[q, lo], right),
            (p0.at[q, 1, hi], fr.at[q, hi], left),
        )[k]
        return pltpu.make_async_remote_copy(src_ref=src, dst_ref=dst, send_sem=rs_send.at[q, k], recv_sem=rs_recv.at[q, k],
                                            device_id={'ep': to}, device_id_type=pl.DeviceIdType.MESH)

    def ag_own(m):
        for k in range(5):
            ag(m, k).start()

    def ag_relay(m):
        ag(m, 0).wait_recv()
        ag(m, 5).start()
        ag(m, 2).wait_recv()
        ag(m, 6).start()

    def ag_share(m):
        ag(m, 1).wait_recv()
        ag(m, 7).start()
        ag(m, 3).wait_recv()
        ag(m, 8).start()

    def ag_share_far(m):
        ag(m, 5).wait_recv()
        ag(m, 9).start()
        ag(m, 6).wait_recv()
        ag(m, 10).start()

    lane = lax.broadcasted_iota(jnp.int32, (local_n, n_slot), 1)
    owner = lax.broadcasted_iota(jnp.int32, (local_n, n_slot), 0)
    spread = jnp.where((lane >= owner * cap2) & (lane < (owner + 1) * cap2), 1.0, 0.0).astype(F32)

    def place(m, o):
        ids = lax.broadcasted_iota(jnp.int32, (local_n, tok_n), 0).astype(F32) + first
        tri = jnp.where(lax.broadcasted_iota(jnp.int32, (tok_n, tok_n), 0) < lax.broadcasted_iota(jnp.int32, (tok_n, tok_n), 1),
                        1.0, 0.0).astype(BF16)
        slot_parts, gate_parts = [], []
        for j in range(2):
            member = jnp.zeros((local_n, tok_n), F32)
            gate = jnp.zeros((local_n, tok_n), F32)
            for t in range(top_k):
                hit = mbuf[o, j, 16 * m + t:16 * m + t + 1, :] == ids
                member = jnp.where(hit, 1.0, member)
                gate = jnp.where(hit, mbuf[o, j, 16 * m + 8 + t:16 * m + 9 + t, :], gate)
            rank = jnp.dot(member.astype(BF16), tri, preferred_element_type=F32)
            slot_parts.append(jnp.where(member > 0.5, rank + float(j * cap), -1.0))
            gate_parts.append(gate)
        slot = jnp.concatenate(slot_parts, axis=1)
        gate = jnp.concatenate(gate_parts, axis=1)
        slots[...] = slot
        index = lax.broadcasted_iota(jnp.int32, (cap2, 2 * tok_n), 0).astype(F32)
        sel = jnp.concatenate([jnp.where(index == slots[e:e + 1, :], 1.0, 0.0) for e in range(local_n)], axis=0).astype(BF16)
        wide = 2 * WIDE
        both = xbuf[o].reshape(2 * tok_n, dim)
        for k in range(0, dim, wide):
            n = min(wide, dim - k)
            got = jnp.dot(sel, both[:, k:k + n], preferred_element_type=F32).astype(BF16)
            for e in range(local_n):
                rows[e, o * cap2:(o + 1) * cap2, k:k + n] = got[e * cap2:(e + 1) * cap2, :]

        def over(a):
            return lax.dot_general(a, spread, (((0,), (0,)), ((), ())), preferred_element_type=F32)

        pos = lax.broadcasted_iota(jnp.int32, (2 * tok_n, n_slot), 1)
        pos = lax.rem(pos, cap2).astype(F32)
        here = over(slot) == pos
        rest = gate
        for part in range(3):
            head = rest.astype(BF16).astype(F32)
            gts[o, part] = jnp.where(here, over(head), 0.0).astype(BF16)
            rest = rest - head

    def gate_up(base, kinds, events):
        def step(i, carry):
            at = base + 2 * i
            e, f = i // n_f, i % n_f
            tall_copy(wo_ref.at[:, pl.ds(0, WIDE)], at).wait()
            tall_copy(wo_ref.at[:, pl.ds(0, WIDE)], at + 1).wait()
            mine = rows[e]
            gate = jnp.dot(mine, ring[lax.rem(at, RING)], preferred_element_type=F32)
            up = jnp.dot(mine, ring[lax.rem(at + 1, RING)], preferred_element_type=F32)
            hidden[e, :, cols(f)] = (jax.nn.silu(gate) * up).astype(BF16)
            fetch(at + RING, kinds)
            fetch(at + 1 + RING, kinds)
            for when, event in events:
                @pl.when(i == when)
                def _():
                    event()
            return carry

        lax.fori_loop(0, n_gu, step, 0)

    def stage1(q):
        rs(0, q).wait_recv()
        for o in (3, 2, 1, 0):
            p0[q, o] = p0[q, o] + dr[q, o]
        for k in (1, 2, 3, 4):
            rs(k, q).start()

    def stage2(q):
        rs(1, q).wait_recv()
        rs(2, q).wait_recv()
        p0[q, 2, lo] = p0[q, 2, lo] + ri[q, 0]
        p0[q, 1, hi] = p0[q, 1, hi] + ri[q, 1]
        rs(5, q).start()
        rs(6, q).start()

    def combine(q):
        for o in range(n_pair):
            total = None
            for part in range(3):
                term = jnp.dot(gts[o, part], ys[o], preferred_element_type=F32)
                total = term if total is None else total + term
            p1[lax.rem(q, 2), o] = total[tok_n:, :]
            p0[q, o] = total[:tok_n, :]

    def down(m, base, kinds):
        def step(i, carry):
            at = base + i
            q, e = i // local_n, i % local_n
            down_copy(0, 0, at).wait()
            y = jnp.dot(hidden[e], ring[lax.rem(at, RING), pl.ds(0, ff)], preferred_element_type=F32).astype(BF16)
            for o in range(n_pair):
                ys[o, pl.ds(pl.multiple_of(e * cap2, 16), cap2), :] = y[o * cap2:(o + 1) * cap2, :]
            fetch(at + RING, kinds)

            @pl.when((e == 4) & (q >= 1))
            def _():
                stage1(q - 1)

            @pl.when((e == 1) & (q >= 2))
            def _():
                stage2(q - 2)

            @pl.when(e == local_n - 1)
            def _():
                @pl.when(q >= 2)
                def _():
                    rs(0, q - 2).wait_send()
                combine(q)
                if m == 1:
                    @pl.when(q == 0)
                    def _():
                        pl.semaphore_wait(rs_free, len(peers))
                rs(0, q).start()
            return carry

        lax.fori_loop(0, n_d, step, 0)

    def finish(m):
        tokens, out = (x_ref, outa_ref) if m == 0 else (ubuf, outb_ref)

        def step(q, carry):
            for k in (3, 4, 5, 6):
                rs(k, q).wait_recv()
            total = p0[q, 0] + fl[q] + fr[q]
            out[:, cols(q)] = (tokens[:, cols(q)].astype(F32) + total).astype(BF16)
            return carry

        lax.fori_loop(0, n_q, step, 0)

        def drain(q, carry):
            for k in (1, 2, 3, 4, 5, 6):
                rs(k, q).wait_send()
            return carry

        lax.fori_loop(0, n_q, drain, 0)
        for q in (n_q - 2, n_q - 1):
            rs(0, q).wait_send()

    for idx in range(RING):
        fetch(idx, ('o', 'ga'))
    barrier = pltpu.get_barrier_semaphore()
    signal_peers(barrier)
    pl.semaphore_wait(barrier, len(peers))
    for k in (0, 1, 2):
        meta(k).start()
    ag_own(0)
    mbuf[0, 0] = meta_ref[...]
    xbuf[0, 0] = x_ref[...]

    def project(i, carry):
        proj = jnp.dot(attn_ref[...], tall(i), preferred_element_type=F32).astype(BF16)
        ubuf[:, cols(i)] = (h_ref[:, cols(i)].astype(F32) + proj.astype(F32)).astype(BF16)
        fetch(i + RING, ('ga',))
        return carry

    lax.fori_loop(0, n_o, project, 0)
    meta(0).wait_recv()
    meta(3).start()
    meta(4).start()
    meta(1).wait_recv()
    meta(5).start()
    meta(2).wait_recv()
    ag(0, 4).wait_recv()
    place(0, 0)
    ag_relay(0)
    meta(3).wait_recv()
    meta(6).start()
    for k in (4, 5, 6):
        meta(k).wait_recv()
    ag_share(0)
    ag(0, 7).wait_recv()
    place(0, 1)
    ag(0, 8).wait_recv()
    place(0, 2)
    ag_share_far(0)
    ag(0, 9).wait_recv()
    ag(0, 10).wait_recv()
    place(0, 3)
    for k in range(11):
        ag(0, k).wait_send()
    for k in range(7):
        meta(k).wait_send()
    signal_peers(x_free)

    def send_b():
        pl.semaphore_wait(x_free, len(peers))
        ag_own(1)
        xbuf[0, 0] = ubuf[...]

    gate_up(at_ga, ('ga', 'da'), (
        (1, send_b),
        (8, lambda: ag_relay(1)),
        (13, lambda: ag_share(1)),
        (18, lambda: ag_share_far(1)),
    ))
    down(0, at_da, ('da', 'gb'))
    for k in (4, 7, 8, 9, 10):
        ag(1, k).wait_recv()
    for o in range(n_pair):
        place(1, o)
        if o == 1:
            stage1(n_q - 1)
    gate_up(at_gb, ('gb', 'db'), (
        (1, lambda: stage2(n_q - 2)),
        (5, lambda: stage2(n_q - 1)),
    ))
    finish(0)
    signal_peers(rs_free)
    down(1, at_db, ('db', 'w'))

    def qkv(i, carry):
        qkv_ref[:, cols(i)] = jnp.dot(h_ref[...], tall(at_w + i), preferred_element_type=F32).astype(BF16)

        @pl.when(i == 2)
        def _():
            stage1(n_q - 1)

        @pl.when(i == 3)
        def _():
            stage2(n_q - 2)
        return carry

    lax.fori_loop(0, n_w, qkv, 0)
    stage2(n_q - 1)
    finish(1)
    for k in range(11):
        ag(1, k).wait_send()


def solution(mesh):
    n_devs = mesh.shape['ep']

    def local_step(x_a, route_a, gate_a, h_b, attn_b, route_b, gate_b, w_qkv, w_o, w_gate, w_up, w_down):
        tok_n, dim = x_a.shape
        top_k = route_a.shape[1]
        local_n, _, ff = w_gate.shape
        qkv_n = w_qkv.shape[1]
        n_experts = local_n * n_devs
        cap = min(tok_n, 2 * ((tok_n * top_k + n_experts - 1) // n_experts))
        n_pair = n_devs // 2
        n_q = dim // WIDE
        cap2 = 2 * cap
        m = n_pair * cap2
        half = tok_n // 2

        def eight(a):
            return jnp.concatenate([a.astype(F32).T, jnp.full((8 - top_k, tok_n), -1.0, F32)], axis=0)

        meta = jnp.concatenate([eight(route_a), eight(gate_a), eight(route_b), eight(gate_b)], axis=0)
        vmem = pl.BlockSpec(memory_space=pltpu.VMEM)
        hbm = pl.BlockSpec(memory_space=pl.ANY)
        flops = 2 * 2 * 3 * local_n * m * dim * ff
        weight_bytes = 2 * 6 * local_n * dim * ff
        return pl.pallas_call(
            functools.partial(moe_kernel, n_devs, top_k, cap),
            out_shape=(
                jax.ShapeDtypeStruct((tok_n, dim), BF16),
                jax.ShapeDtypeStruct((tok_n, dim), BF16),
                jax.ShapeDtypeStruct((tok_n, qkv_n), BF16),
            ),
            in_specs=[vmem] * 4 + [hbm] * 5,
            out_specs=(vmem, vmem, vmem),
            scratch_shapes=[
                pltpu.VMEM((RING, dim, WIDE), BF16),
                pltpu.VMEM((n_pair, 2, tok_n, dim), BF16),
                pltpu.VMEM((n_pair, 2, 32, tok_n), F32),
                pltpu.VMEM((tok_n, dim), BF16),
                pltpu.VMEM((local_n, m, dim), BF16),
                pltpu.VMEM((local_n, m, ff), BF16),
                pltpu.VMEM((local_n, 2 * tok_n), F32),
                pltpu.VMEM((n_pair, 3, 2 * tok_n, local_n * cap2), BF16),
                pltpu.VMEM((n_pair, local_n * cap2, WIDE), BF16),
                pltpu.VMEM((n_q, n_pair, tok_n, WIDE), F32),
                pltpu.VMEM((2, n_pair, tok_n, WIDE), F32),
                pltpu.VMEM((n_q, n_pair, tok_n, WIDE), F32),
                pltpu.VMEM((n_q, 2, half, WIDE), F32),
                pltpu.VMEM((n_q, tok_n, WIDE), F32),
                pltpu.VMEM((n_q, tok_n, WIDE), F32),
                pltpu.SemaphoreType.DMA((RING,)),
                pltpu.SemaphoreType.DMA((2, 11)),
                pltpu.SemaphoreType.DMA((2, 11)),
                pltpu.SemaphoreType.DMA((7,)),
                pltpu.SemaphoreType.DMA((7,)),
                pltpu.SemaphoreType.DMA((n_q, 7)),
                pltpu.SemaphoreType.DMA((n_q, 7)),
                pltpu.SemaphoreType.REGULAR,
                pltpu.SemaphoreType.REGULAR,
            ],
            compiler_params=pltpu.CompilerParams(collective_id=0, has_side_effects=True, vmem_limit_bytes=67043328),
            cost_estimate=pl.CostEstimate(flops=flops, bytes_accessed=weight_bytes, transcendentals=0),
        )(x_a, h_b, attn_b, meta, w_qkv, w_o, w_gate, w_up, w_down)

    row_spec = P(('dp', 'ep'), None)
    full_spec = P(None, None)
    expert_spec = P('ep', None, None)
    return jax.shard_map(
        local_step,
        mesh=mesh,
        in_specs=(row_spec, row_spec, row_spec, row_spec, row_spec, row_spec, row_spec, full_spec, full_spec, expert_spec, expert_spec, expert_spec),
        out_specs=(row_spec, row_spec, row_spec),
        check_vma=False,
    )
```

time: 443 us -> 209 us (0.47); the launches traced: 434 us -> 209 us
  matrix products: 206 us -> 0 us
  Pallas kernels: 0 us -> 198 us
  waiting for transfers between devices: 143 us -> 0 us
  local copies, waits for them, and re-layouts: 51.5 us -> 9.88 us
  starting transfers between devices: 23.3 us -> 0 us
  other arithmetic: 9.32 us -> 0.71 us
    dot_general x10 -> x0, matrix products: 206 us -> none  [the longest x2 107 us: expert_ffn(): jnp.einsum('erf,efd->erd', hidden, w_down, preferred_element_type=jnp.flo...]
    pallas_call x0 -> x1, Pallas kernels: none -> 198 us  [local_step(): pl.pallas_call(functools.partial(moe_kernel, n_devs, top_k, cap), out_sha...]
    all_to_all x4 -> x0, waiting for transfers between devices: 143 us -> none  [the longest x2 77.7 us: moe_local(): recv_buf = lax.all_to_all(send_buf, 'ep', 1, 1, tiled=True)]
    all_to_all x4 -> x0, local copies, waits for them, and re-layouts: 25.3 us -> none  [the longest x2 14.2 us: moe_local(): recv_buf = lax.all_to_all(send_buf, 'ep', 1, 1, tiled=True)]
    all_to_all x4 -> x0, starting transfers between devices: 23.3 us -> none  [the longest x2 12.3 us: moe_local(): recv_buf = lax.all_to_all(send_buf, 'ep', 1, 1, tiled=True)]
    reshape x4 -> x0, local copies, waits for them, and re-layouts: 21.7 us -> none  [the longest x2 14.1 us: moe_local(): expert_out.reshape(local_n, n_devs, capacity, model_dim)]
  transfers between devices with their start and end apart: 4 -> 0, of which waited for: 2 -> 0; matrix products, arithmetic and copies ran while one was open for 52% -> 0% of each run, Pallas kernels for 0% -> 0%
where the time goes in v2:
time: 209 us
  Pallas kernels  198 us (95%)
  local copies, waits for them, and re-layouts  9.88 us (5%)
    pallas_call x1, Pallas kernels, local_step(): pl.pallas_call(functools.partial(moe_kernel, n_devs, top_k, cap), out_sha...  198 us
    unnamed x3, local copies, waits for them, and re-layouts  6.09 us

profile of v2, /device:TPU:113, one launch (start us, length us, event | category | flops | bytes accessed | tf_op | source)
XLA Modules:
  0.0 209.1 jit_solution(555704907452590931)
XLA Ops:
  0.6 0.7 convert_bitcast_fusion
  1.3 3.8 %concatenate.3.meta_ref = f32[32,128]{1,0:T(8,128)} concatenate(f32[6,128]{1,0:T(8,128)S(1)} %get-tuple-element.4, f32[2,128]{1,0:T(2,128)S(1)} %broadcast.3, f32[6,128]{1,0:T(8,128)} %bitcast.6, f32[2,128]{1,0:T(2,128)S(1)} %broadcast.3, f32[6,128]{1,0:T(8,128)S(1)} %get-tuple-element.3, f32[2,128]{1,0:T(2,128)S(1)} %broadcast.3, f32[6,128]{1,0:T(8,128)} %bitcast.7, ...), dimensions={0} | concatenate | bytes 32768 | tf_op jit(solution)/shard_map/concatenate | solution.py:416
  5.1 197.9 %shard_map.139 = (bf16[128,2560]{1,0:T(8,128)(2,1)}, bf16[128,2560]{1,0:T(8,128)(2,1)}, bf16[128,3584]{1,0:T(8,128)(2,1)}) custom-call(bf16[128,2560]{1,0:T(8,128)(2,1)} %x_ref.1, bf16[128,2560]{1,0:T(8,128)(2,1)} %h_ref.1, bf16[128,2560]{1,0:T(8,128)(2,1)} %attn_ref.1, f32[32,128]{1,0:T(8,128)} %concatenate.3.meta_ref, bf16[2560,3584]{1,0:T(8,128)(2,1)} %wqkv_ref.1, ...), custom_call_target="tpu_custom_call" | custom-call | flops 72477573120 | bytes 377487360 | tf_op jit(solution)/shard_map/pallas_call | solution.py:421
  203.0 2.0 copy.18
  205.0 2.0 copy.19
  206.9 2.2 %copy.20 = bf16[128,3584]{1,0:T(8,128)(2,1)} copy(bf16[128,3584]{1,0:T(8,128)(2,1)} %get-tuple-element.10) | data formatting | bytes 1835008
  (1 shorter events, 0.0 us)

commit v3 on v2

--- a/solution.py
+++ b/solution.py
@@ -13,7 +13,7 @@
 WIDE = 512
 
 
-def moe_kernel(n_devs, top_k, cap, x_ref, h_ref, attn_ref, meta_ref, wqkv_ref, wo_ref, wg_ref, wu_ref, wd_ref,
+def moe_kernel(n_devs, top_k, cap, x_ref, h_ref, attn_ref, ra_ref, ga_ref, rb_ref, gb_ref, wqkv_ref, wo_ref, wg_ref, wu_ref, wd_ref,
                outa_ref, outb_ref, qkv_ref,
                ring, xbuf, mbuf, ubuf, rows, hidden, slots, gts, ys, p0, p1, dr, ri, fl, fr,
                ring_sem, ag_send, ag_recv, me_send, me_recv, rs_send, rs_recv, x_free, rs_free):
@@ -23,7 +23,7 @@
     qkv_n = wqkv_ref.shape[1]
     cap2 = 2 * cap
     n_pair = n_devs // 2
-    n_slot = local_n * cap2
+    n_slot = local_n * cap
     me = lax.axis_index('ep')
     core = lax.rem(me, 2)
     partner = me + 1 - 2 * core
@@ -115,9 +115,9 @@
 
     def meta(k):
         src, dst, to = (
-            (meta_ref, mbuf.at[1, 0], right),
-            (meta_ref, mbuf.at[2, 0], left),
-            (meta_ref, mbuf.at[0, 1], partner),
+            (mbuf.at[0, 0], mbuf.at[1, 0], right),
+            (mbuf.at[0, 0], mbuf.at[2, 0], left),
+            (mbuf.at[0, 0], mbuf.at[0, 1], partner),
             (mbuf.at[1, 0], mbuf.at[3, 0], right),
             (mbuf.at[1, 0], mbuf.at[1, 1], partner),
             (mbuf.at[2, 0], mbuf.at[2, 1], partner),
@@ -163,13 +163,17 @@
 
     lane = lax.broadcasted_iota(jnp.int32, (local_n, n_slot), 1)
     owner = lax.broadcasted_iota(jnp.int32, (local_n, n_slot), 0)
-    spread = jnp.where((lane >= owner * cap2) & (lane < (owner + 1) * cap2), 1.0, 0.0).astype(F32)
+    spread = jnp.where((lane >= owner * cap) & (lane < (owner + 1) * cap), 1.0, 0.0).astype(F32)
 
     def place(m, o):
         ids = lax.broadcasted_iota(jnp.int32, (local_n, tok_n), 0).astype(F32) + first
         tri = jnp.where(lax.broadcasted_iota(jnp.int32, (tok_n, tok_n), 0) < lax.broadcasted_iota(jnp.int32, (tok_n, tok_n), 1),
                         1.0, 0.0).astype(BF16)
-        slot_parts, gate_parts = [], []
+        pos = lax.rem(lax.broadcasted_iota(jnp.int32, (tok_n, n_slot), 1), cap).astype(F32)
+
+        def over(a):
+            return lax.dot_general(a, spread, (((0,), (0,)), ((), ())), preferred_element_type=F32)
+
         for j in range(2):
             member = jnp.zeros((local_n, tok_n), F32)
             gate = jnp.zeros((local_n, tok_n), F32)
@@ -178,11 +182,13 @@
                 member = jnp.where(hit, 1.0, member)
                 gate = jnp.where(hit, mbuf[o, j, 16 * m + 8 + t:16 * m + 9 + t, :], gate)
             rank = jnp.dot(member.astype(BF16), tri, preferred_element_type=F32)
-            slot_parts.append(jnp.where(member > 0.5, rank + float(j * cap), -1.0))
-            gate_parts.append(gate)
-        slot = jnp.concatenate(slot_parts, axis=1)
-        gate = jnp.concatenate(gate_parts, axis=1)
-        slots[...] = slot
+            slots[:, j * tok_n:(j + 1) * tok_n] = jnp.where(member > 0.5, rank + float(j * cap), -1.0)
+            here = over(jnp.where(member > 0.5, rank, -1.0)) == pos
+            rest = gate
+            for part in range(3):
+                head = rest.astype(BF16).astype(F32)
+                gts[o, j, part] = jnp.where(here, over(head), 0.0).astype(BF16)
+                rest = rest - head
         index = lax.broadcasted_iota(jnp.int32, (cap2, 2 * tok_n), 0).astype(F32)
         sel = jnp.concatenate([jnp.where(index == slots[e:e + 1, :], 1.0, 0.0) for e in range(local_n)], axis=0).astype(BF16)
         wide = 2 * WIDE
@@ -192,18 +198,6 @@
             got = jnp.dot(sel, both[:, k:k + n], preferred_element_type=F32).astype(BF16)
             for e in range(local_n):
                 rows[e, o * cap2:(o + 1) * cap2, k:k + n] = got[e * cap2:(e + 1) * cap2, :]
-
-        def over(a):
-            return lax.dot_general(a, spread, (((0,), (0,)), ((), ())), preferred_element_type=F32)
-
-        pos = lax.broadcasted_iota(jnp.int32, (2 * tok_n, n_slot), 1)
-        pos = lax.rem(pos, cap2).astype(F32)
-        here = over(slot) == pos
-        rest = gate
-        for part in range(3):
-            head = rest.astype(BF16).astype(F32)
-            gts[o, part] = jnp.where(here, over(head), 0.0).astype(BF16)
-            rest = rest - head
 
     def gate_up(base, kinds, events):
         def step(i, carry):
@@ -217,10 +211,7 @@
             hidden[e, :, cols(f)] = (jax.nn.silu(gate) * up).astype(BF16)
             fetch(at + RING, kinds)
             fetch(at + 1 + RING, kinds)
-            for when, event in events:
-                @pl.when(i == when)
-                def _():
-                    event()
+            events(i)
             return carry
 
         lax.fori_loop(0, n_gu, step, 0)
@@ -242,32 +233,39 @@
 
     def combine(q):
         for o in range(n_pair):
-            total = None
-            for part in range(3):
-                term = jnp.dot(gts[o, part], ys[o], preferred_element_type=F32)
-                total = term if total is None else total + term
-            p1[lax.rem(q, 2), o] = total[tok_n:, :]
-            p0[q, o] = total[:tok_n, :]
+            for j in (1, 0):
+                total = None
+                for part in range(3):
+                    term = jnp.dot(gts[o, j, part], ys[o, j], preferred_element_type=F32)
+                    total = term if total is None else total + term
+                if j == 1:
+                    p1[lax.rem(q, 2), o] = total
+                else:
+                    p0[q, o] = total
 
     def down(m, base, kinds):
+        n_e = local_n // 2
+
         def step(i, carry):
-            at = base + i
-            q, e = i // local_n, i % local_n
+            at = base + 2 * i
+            q, e = i // n_e, i % n_e
             down_copy(0, 0, at).wait()
-            y = jnp.dot(hidden[e], ring[lax.rem(at, RING), pl.ds(0, ff)], preferred_element_type=F32).astype(BF16)
+            down_copy(0, 0, at + 1).wait()
+            y0 = jnp.dot(hidden[2 * e], ring[lax.rem(at, RING), pl.ds(0, ff)], preferred_element_type=F32)
+            y1 = jnp.dot(hidden[2 * e + 1], ring[lax.rem(at + 1, RING), pl.ds(0, ff)], preferred_element_type=F32)
             for o in range(n_pair):
-                ys[o, pl.ds(pl.multiple_of(e * cap2, 16), cap2), :] = y[o * cap2:(o + 1) * cap2, :]
+                for j in range(2):
+                    here = slice(o * cap2 + j * cap, o * cap2 + (j + 1) * cap)
+                    two = jnp.concatenate([y0[here], y1[here]], axis=0)
+                    ys[o, j, pl.ds(pl.multiple_of(e * cap2, 16), cap2), :] = two.astype(BF16)
             fetch(at + RING, kinds)
-
-            @pl.when((e == 4) & (q >= 1))
+            fetch(at + 1 + RING, kinds)
+
+            @pl.when((e == 1) & (q >= 1))
             def _():
                 stage1(q - 1)
 
-            @pl.when((e == 1) & (q >= 2))
-            def _():
-                stage2(q - 2)
-
-            @pl.when(e == local_n - 1)
+            @pl.when(e == n_e - 1)
             def _():
                 @pl.when(q >= 2)
                 def _():
@@ -280,7 +278,7 @@
                 rs(0, q).start()
             return carry
 
-        lax.fori_loop(0, n_d, step, 0)
+        lax.fori_loop(0, n_d // 2, step, 0)
 
     def finish(m):
         tokens, out = (x_ref, outa_ref) if m == 0 else (ubuf, outb_ref)
@@ -307,11 +305,13 @@
         fetch(idx, ('o', 'ga'))
     barrier = pltpu.get_barrier_semaphore()
     signal_peers(barrier)
+    mbuf[0, 0] = jnp.zeros_like(mbuf[0, 0])
+    for at, ref in ((0, ra_ref), (8, ga_ref), (16, rb_ref), (24, gb_ref)):
+        mbuf[0, 0, at:at + top_k, :] = ref[...].astype(F32)
     pl.semaphore_wait(barrier, len(peers))
     for k in (0, 1, 2):
         meta(k).start()
     ag_own(0)
-    mbuf[0, 0] = meta_ref[...]
     xbuf[0, 0] = x_ref[...]
 
     def project(i, carry):
@@ -354,12 +354,13 @@
         ag_own(1)
         xbuf[0, 0] = ubuf[...]
 
-    gate_up(at_ga, ('ga', 'da'), (
-        (1, send_b),
-        (8, lambda: ag_relay(1)),
-        (13, lambda: ag_share(1)),
-        (18, lambda: ag_share_far(1)),
-    ))
+    def during_a(i):
+        for when, event in ((1, send_b), (8, lambda: ag_relay(1)), (13, lambda: ag_share(1)), (18, lambda: ag_share_far(1))):
+            @pl.when(i == when)
+            def _():
+                event()
+
+    gate_up(at_ga, ('ga', 'da'), during_a)
     down(0, at_da, ('da', 'gb'))
     for k in (4, 7, 8, 9, 10):
         ag(1, k).wait_recv()
@@ -367,10 +368,13 @@
         place(1, o)
         if o == 1:
             stage1(n_q - 1)
-    gate_up(at_gb, ('gb', 'db'), (
-        (1, lambda: stage2(n_q - 2)),
-        (5, lambda: stage2(n_q - 1)),
-    ))
+
+    def during_b(i):
+        @pl.when((i % 2 == 1) & (i < 2 * n_q))
+        def _():
+            stage2(i // 2)
+
+    gate_up(at_gb, ('gb', 'db'), during_b)
     finish(0)
     signal_peers(rs_free)
     down(1, at_db, ('db', 'w'))
@@ -378,13 +382,13 @@
     def qkv(i, carry):
         qkv_ref[:, cols(i)] = jnp.dot(h_ref[...], tall(at_w + i), preferred_element_type=F32).astype(BF16)
 
-        @pl.when(i == 2)
+        @pl.when(i == 1)
         def _():
             stage1(n_q - 1)
 
-        @pl.when(i == 3)
+        @pl.when((i >= 2) & (i - 2 < n_q - 1))
         def _():
-            stage2(n_q - 2)
+            stage2(i - 2)
         return carry
 
     lax.fori_loop(0, n_w, qkv, 0)
@@ -392,6 +396,28 @@
     finish(1)
     for k in range(11):
         ag(1, k).wait_send()
+
+
+def write_kernel(a_ref, b_ref, c_ref, oa_ref, ob_ref, oc_ref, va, vb, vc, sem_in, sem_out):
+    moves = ((a_ref, va, oa_ref), (b_ref, vb, ob_ref), (c_ref, vc, oc_ref))
+    for k, (src, buf, _) in enumerate(moves):
+        pltpu.make_async_copy(src, buf, sem_in.at[k]).start()
+    for k, (src, buf, dst) in enumerate(moves):
+        pltpu.make_async_copy(src, buf, sem_in.at[k]).wait()
+        pltpu.make_async_copy(buf, dst, sem_out.at[k]).start()
+    for k, (_, buf, dst) in enumerate(moves):
+        pltpu.make_async_copy(buf, dst, sem_out.at[k]).wait()
+
+
+def write_out(arrays):
+    hbm = pl.BlockSpec(memory_space=pl.ANY)
+    return pl.pallas_call(
+        write_kernel,
+        out_shape=tuple(jax.ShapeDtypeStruct(a.shape, a.dtype) for a in arrays),
+        in_specs=[hbm] * 3,
+        out_specs=(hbm,) * 3,
+        scratch_shapes=[pltpu.VMEM(a.shape, a.dtype) for a in arrays] + [pltpu.SemaphoreType.DMA((3,)), pltpu.SemaphoreType.DMA((3,))],
+    )(*arrays)
 
 
 def solution(mesh):
@@ -410,22 +436,18 @@
         m = n_pair * cap2
         half = tok_n // 2
 
-        def eight(a):
-            return jnp.concatenate([a.astype(F32).T, jnp.full((8 - top_k, tok_n), -1.0, F32)], axis=0)
-
-        meta = jnp.concatenate([eight(route_a), eight(gate_a), eight(route_b), eight(gate_b)], axis=0)
         vmem = pl.BlockSpec(memory_space=pltpu.VMEM)
         hbm = pl.BlockSpec(memory_space=pl.ANY)
         flops = 2 * 2 * 3 * local_n * m * dim * ff
         weight_bytes = 2 * 6 * local_n * dim * ff
-        return pl.pallas_call(
+        results = pl.pallas_call(
             functools.partial(moe_kernel, n_devs, top_k, cap),
             out_shape=(
                 jax.ShapeDtypeStruct((tok_n, dim), BF16),
                 jax.ShapeDtypeStruct((tok_n, dim), BF16),
                 jax.ShapeDtypeStruct((tok_n, qkv_n), BF16),
             ),
-            in_specs=[vmem] * 4 + [hbm] * 5,
+            in_specs=[vmem] * 7 + [hbm] * 5,
             out_specs=(vmem, vmem, vmem),
             scratch_shapes=[
                 pltpu.VMEM((RING, dim, WIDE), BF16),
@@ -435,8 +457,8 @@
                 pltpu.VMEM((local_n, m, dim), BF16),
                 pltpu.VMEM((local_n, m, ff), BF16),
                 pltpu.VMEM((local_n, 2 * tok_n), F32),
-                pltpu.VMEM((n_pair, 3, 2 * tok_n, local_n * cap2), BF16),
-                pltpu.VMEM((n_pair, local_n * cap2, WIDE), BF16),
+                pltpu.VMEM((n_pair, 2, 3, tok_n, local_n * cap), BF16),
+                pltpu.VMEM((n_pair, 2, local_n * cap, WIDE), BF16),
                 pltpu.VMEM((n_q, n_pair, tok_n, WIDE), F32),
                 pltpu.VMEM((2, n_pair, tok_n, WIDE), F32),
                 pltpu.VMEM((n_q, n_pair, tok_n, WIDE), F32),
@@ -455,7 +477,8 @@
             ],
             compiler_params=pltpu.CompilerParams(collective_id=0, has_side_effects=True, vmem_limit_bytes=67043328),
             cost_estimate=pl.CostEstimate(flops=flops, bytes_accessed=weight_bytes, transcendentals=0),
-        )(x_a, h_b, attn_b, meta, w_qkv, w_o, w_gate, w_up, w_down)
+        )(x_a, h_b, attn_b, route_a.T, gate_a.T, route_b.T, gate_b.T, w_qkv, w_o, w_gate, w_up, w_down)
+        return write_out(results)
 
     row_spec = P(('dp', 'ep'), None)
     full_spec = P(None, None)

time: 209 us -> 188 us (0.90)
  Pallas kernels: 198 us -> 187 us
  local copies, waits for them, and re-layouts: 9.88 us -> 0 us
    pallas_call x1, Pallas kernels: 198 us -> 184 us  [local_step(): pl.pallas_call(functools.partial(moe_kernel, n_devs, top_k, cap), out_sha...]
    unnamed x3 -> x0, local copies, waits for them, and re-layouts: 6.09 us -> none
    concatenate x1 -> x0, local copies, waits for them, and re-layouts: 3.79 us -> none  [local_step(): jnp.concatenate([eight(route_a), eight(gate_a), eight(route_b), eight(gat...]
    pallas_call x0 -> x1, Pallas kernels: none -> 2.55 us  [write_out(): pl.pallas_call(write_kernel, out_shape=tuple((jax.ShapeDtypeStruct(a.shap...]
where the time goes in v3:
time: 188 us; the launch traced here: 187 us
  Pallas kernels  187 us (99%)
    pallas_call x1, Pallas kernels, local_step(): pl.pallas_call(functools.partial(moe_kernel, n_devs, top_k, cap), out_sha...  184 us

profile of v3, /device:TPU:113, one launch (start us, length us, event | category | flops | bytes accessed | tf_op | source)
XLA Modules:
  0.0 187.4 jit_solution(504110388930015636)
XLA Ops:
  0.6 184.2 %shard_map.139 = (bf16[128,2560]{1,0:T(8,128)(2,1)}, bf16[128,2560]{1,0:T(8,128)(2,1)}, bf16[128,3584]{1,0:T(8,128)(2,1)}) custom-call(bf16[128,2560]{1,0:T(8,128)(2,1)} %x_ref.1, bf16[128,2560]{1,0:T(8,128)(2,1)} %h_ref.1, bf16[128,2560]{1,0:T(8,128)(2,1)} %attn_ref.1, s32[6,128]{1,0:T(8,128)} %bitcast.4, f32[6,128]{1,0:T(8,128)} %bitcast.5, ...), custom_call_target="tpu_custom_call" | custom-call | flops 72477573120 | bytes 377487360 | tf_op jit(solution)/shard_map/pallas_call | solution.py:443
  184.9 2.6 %shard_map.140 = (bf16[128,2560]{1,0:T(8,128)(2,1)}, bf16[128,2560]{1,0:T(8,128)(2,1)}, bf16[128,3584]{1,0:T(8,128)(2,1)}) custom-call(bf16[128,2560]{1,0:T(8,128)(2,1)} %get-tuple-element.6.a_ref, bf16[128,2560]{1,0:T(8,128)(2,1)} %get-tuple-element.7.b_ref, bf16[128,3584]{1,0:T(8,128)(2,1)} %get-tuple-element.8.c_ref), custom_call_target="tpu_custom_call" | custom-call | tf_op jit(solution)/shard_map/pallas_call | solution.py:414

commit v4 on v3

--- a/solution.py
+++ b/solution.py
@@ -11,12 +11,14 @@
 BF16 = jnp.bfloat16
 RING = 8
 WIDE = 512
-
-
-def moe_kernel(n_devs, top_k, cap, x_ref, h_ref, attn_ref, ra_ref, ga_ref, rb_ref, gb_ref, wqkv_ref, wo_ref, wg_ref, wu_ref, wd_ref,
+SHARED = 2
+
+
+def moe_kernel(n_devs, top_k, cap, ra_ref, ga_ref, rb_ref, gb_ref, x_ref, h_ref, attn_ref,
+               wqkv_ref, wo_ref, wg_ref, wu_ref, wd_ref,
                outa_ref, outb_ref, qkv_ref,
-               ring, xbuf, mbuf, ubuf, rows, hidden, slots, gts, ys, p0, p1, dr, ri, fl, fr,
-               ring_sem, ag_send, ag_recv, me_send, me_recv, rs_send, rs_recv, x_free, rs_free):
+               ring, xbuf, mbuf, ubuf, abuf, bbuf, hbuf, qbuf, rows, hidden, later, slots, gts, ys, p0, p1, dr, ri, fl, fr,
+               ring_sem, io_sem, ag_send, ag_recv, me_send, me_recv, rs_send, rs_recv, x_free, rs_free):
     tok_n, dim = x_ref.shape
     half = tok_n // 2
     local_n, _, ff = wg_ref.shape
@@ -37,11 +39,11 @@
             pl.semaphore_signal(sem, inc=1, device_id={'ep': peer}, device_id_type=pl.DeviceIdType.MESH)
 
     n_o, n_f, n_q, n_w = dim // WIDE, ff // WIDE, dim // WIDE, qkv_n // WIDE
-    n_gu, n_d = local_n * n_f, local_n * n_q
+    n_ga, n_gb, n_d = local_n * n_f, (local_n - SHARED) * n_f, local_n * n_q
     at_ga = n_o
-    at_da = at_ga + 2 * n_gu
+    at_da = at_ga + 2 * n_ga
     at_gb = at_da + n_d
-    at_db = at_gb + 2 * n_gu
+    at_db = at_gb + 2 * n_gb
     at_w = at_db + n_d
     at_end = at_w + n_w
 
@@ -73,9 +75,9 @@
             @pl.when(idx < at_ga)
             def _():
                 tall_copy(wo_ref.at[:, cols(idx)], idx).start()
-        for name, base in (('ga', at_ga), ('gb', at_gb)):
+        for name, base, steps in (('ga', at_ga, n_ga), ('gb', at_gb, n_gb)):
             if name in kinds:
-                @pl.when((idx >= base) & (idx < base + 2 * n_gu))
+                @pl.when((idx >= base) & (idx < base + 2 * steps))
                 def _():
                     start_gu(idx - base, idx)
         for name, base in (('da', at_da), ('db', at_db)):
@@ -96,7 +98,7 @@
     lo, hi = pl.ds(0, half), pl.ds(half, half)
 
     def ag(m, k):
-        own = x_ref if m == 0 else ubuf
+        own = xbuf.at[0, 0] if m == 0 else ubuf
         src, dst, to = (
             (own.at[lo], xbuf.at[1, 0, lo], right),
             (own.at[hi], xbuf.at[1, 0, hi], right),
@@ -165,56 +167,71 @@
     owner = lax.broadcasted_iota(jnp.int32, (local_n, n_slot), 0)
     spread = jnp.where((lane >= owner * cap) & (lane < (owner + 1) * cap), 1.0, 0.0).astype(F32)
 
-    def place(m, o):
+    def member_gate(m, o, j):
         ids = lax.broadcasted_iota(jnp.int32, (local_n, tok_n), 0).astype(F32) + first
+        member = jnp.zeros((local_n, tok_n), F32)
+        gate = jnp.zeros((local_n, tok_n), F32)
+        for t in range(top_k):
+            hit = mbuf[o, j, 16 * m + t:16 * m + t + 1, :] == ids
+            member = jnp.where(hit, 1.0, member)
+            gate = jnp.where(hit, mbuf[o, j, 16 * m + 8 + t:16 * m + 9 + t, :], gate)
+        return member, gate
+
+    def locate(m, o):
         tri = jnp.where(lax.broadcasted_iota(jnp.int32, (tok_n, tok_n), 0) < lax.broadcasted_iota(jnp.int32, (tok_n, tok_n), 1),
                         1.0, 0.0).astype(BF16)
-        pos = lax.rem(lax.broadcasted_iota(jnp.int32, (tok_n, n_slot), 1), cap).astype(F32)
-
-        def over(a):
-            return lax.dot_general(a, spread, (((0,), (0,)), ((), ())), preferred_element_type=F32)
-
         for j in range(2):
-            member = jnp.zeros((local_n, tok_n), F32)
-            gate = jnp.zeros((local_n, tok_n), F32)
-            for t in range(top_k):
-                hit = mbuf[o, j, 16 * m + t:16 * m + t + 1, :] == ids
-                member = jnp.where(hit, 1.0, member)
-                gate = jnp.where(hit, mbuf[o, j, 16 * m + 8 + t:16 * m + 9 + t, :], gate)
+            member, _ = member_gate(m, o, j)
             rank = jnp.dot(member.astype(BF16), tri, preferred_element_type=F32)
-            slots[:, j * tok_n:(j + 1) * tok_n] = jnp.where(member > 0.5, rank + float(j * cap), -1.0)
-            here = over(jnp.where(member > 0.5, rank, -1.0)) == pos
-            rest = gate
-            for part in range(3):
-                head = rest.astype(BF16).astype(F32)
-                gts[o, j, part] = jnp.where(here, over(head), 0.0).astype(BF16)
-                rest = rest - head
+            slots[o, :, j * tok_n:(j + 1) * tok_n] = jnp.where(member > 0.5, rank + float(j * cap), -1.0)
+
+    def take(o, e0, e1):
         index = lax.broadcasted_iota(jnp.int32, (cap2, 2 * tok_n), 0).astype(F32)
-        sel = jnp.concatenate([jnp.where(index == slots[e:e + 1, :], 1.0, 0.0) for e in range(local_n)], axis=0).astype(BF16)
+        sel = jnp.concatenate([jnp.where(index == slots[o, e:e + 1, :], 1.0, 0.0) for e in range(e0, e1)], axis=0).astype(BF16)
         wide = 2 * WIDE
         both = xbuf[o].reshape(2 * tok_n, dim)
         for k in range(0, dim, wide):
             n = min(wide, dim - k)
             got = jnp.dot(sel, both[:, k:k + n], preferred_element_type=F32).astype(BF16)
-            for e in range(local_n):
+            for e in range(e1 - e0):
                 rows[e, o * cap2:(o + 1) * cap2, k:k + n] = got[e * cap2:(e + 1) * cap2, :]
 
-    def gate_up(base, kinds, events):
+    def weigh(m, o):
+        pos = lax.rem(lax.broadcasted_iota(jnp.int32, (tok_n, n_slot), 1), cap).astype(F32)
+
+        def over(a):
+            return lax.dot_general(a, spread, (((0,), (0,)), ((), ())), preferred_element_type=F32)
+
+        for j in range(2):
+            member, rest = member_gate(m, o, j)
+            slot = slots[o, :, j * tok_n:(j + 1) * tok_n]
+            here = over(jnp.where(member > 0.5, slot - float(j * cap), -1.0)) == pos
+            for part in range(3):
+                head = rest.astype(BF16).astype(F32)
+                gts[o, j, part] = jnp.where(here, over(head), 0.0).astype(BF16)
+                rest = rest - head
+
+    def gate_up(base, begin, end, kinds, events, both=False):
+        def act(mine, at):
+            gate = jnp.dot(mine, ring[lax.rem(at, RING)], preferred_element_type=F32)
+            up = jnp.dot(mine, ring[lax.rem(at + 1, RING)], preferred_element_type=F32)
+            return (jax.nn.silu(gate) * up).astype(BF16)
+
         def step(i, carry):
             at = base + 2 * i
             e, f = i // n_f, i % n_f
             tall_copy(wo_ref.at[:, pl.ds(0, WIDE)], at).wait()
             tall_copy(wo_ref.at[:, pl.ds(0, WIDE)], at + 1).wait()
-            mine = rows[e]
-            gate = jnp.dot(mine, ring[lax.rem(at, RING)], preferred_element_type=F32)
-            up = jnp.dot(mine, ring[lax.rem(at + 1, RING)], preferred_element_type=F32)
-            hidden[e, :, cols(f)] = (jax.nn.silu(gate) * up).astype(BF16)
+            hidden[e, :, cols(f)] = act(rows[e], at)
+            if both:
+                k = e - (local_n - SHARED)
+                later[k, :, cols(f)] = act(rows[k], at)
             fetch(at + RING, kinds)
             fetch(at + 1 + RING, kinds)
             events(i)
             return carry
 
-        lax.fori_loop(0, n_gu, step, 0)
+        lax.fori_loop(begin, end, step, 0)
 
     def stage1(q):
         rs(0, q).wait_recv()
@@ -261,6 +278,13 @@
             fetch(at + RING, kinds)
             fetch(at + 1 + RING, kinds)
 
+            if m == 1:
+                @pl.when(e == 0)
+                def _():
+                    finish(0, q)
+                    for peer in peers:
+                        pl.semaphore_signal(rs_free.at[q], inc=1, device_id={'ep': peer}, device_id_type=pl.DeviceIdType.MESH)
+
             @pl.when((e == 1) & (q >= 1))
             def _():
                 stage1(q - 1)
@@ -272,35 +296,35 @@
                     rs(0, q - 2).wait_send()
                 combine(q)
                 if m == 1:
-                    @pl.when(q == 0)
-                    def _():
-                        pl.semaphore_wait(rs_free, len(peers))
+                    pl.semaphore_wait(rs_free.at[q], len(peers))
                 rs(0, q).start()
             return carry
 
         lax.fori_loop(0, n_d // 2, step, 0)
 
-    def finish(m):
-        tokens, out = (x_ref, outa_ref) if m == 0 else (ubuf, outb_ref)
-
-        def step(q, carry):
-            for k in (3, 4, 5, 6):
-                rs(k, q).wait_recv()
-            total = p0[q, 0] + fl[q] + fr[q]
-            out[:, cols(q)] = (tokens[:, cols(q)].astype(F32) + total).astype(BF16)
-            return carry
-
-        lax.fori_loop(0, n_q, step, 0)
-
-        def drain(q, carry):
-            for k in (1, 2, 3, 4, 5, 6):
-                rs(k, q).wait_send()
-            return carry
-
-        lax.fori_loop(0, n_q, drain, 0)
-        for q in (n_q - 2, n_q - 1):
-            rs(0, q).wait_send()
-
+    def finish(m, q):
+        for k in (3, 4, 5, 6):
+            rs(k, q).wait_recv()
+        total = p0[q, 0] + fl[q] + fr[q]
+        tokens, out = (abuf, abuf) if m == 0 else (ubuf, bbuf)
+        out[:, cols(q)] = (tokens[:, cols(q)].astype(F32) + total).astype(BF16)
+        for k in (1, 2, 3, 4, 5, 6):
+            rs(k, q).wait_send()
+
+    def io(k):
+        src, dst = (
+            (x_ref, xbuf.at[0, 0]),
+            (attn_ref, bbuf),
+            (h_ref, hbuf),
+            (x_ref, abuf),
+            (abuf, outa_ref),
+            (bbuf, outb_ref),
+            (qbuf, qkv_ref),
+        )[k]
+        return pltpu.make_async_copy(src, dst, io_sem.at[k])
+
+    for k in range(3):
+        io(k).start()
     for idx in range(RING):
         fetch(idx, ('o', 'ga'))
     barrier = pltpu.get_barrier_semaphore()
@@ -308,15 +332,18 @@
     mbuf[0, 0] = jnp.zeros_like(mbuf[0, 0])
     for at, ref in ((0, ra_ref), (8, ga_ref), (16, rb_ref), (24, gb_ref)):
         mbuf[0, 0, at:at + top_k, :] = ref[...].astype(F32)
+    io(0).wait()
     pl.semaphore_wait(barrier, len(peers))
     for k in (0, 1, 2):
         meta(k).start()
     ag_own(0)
-    xbuf[0, 0] = x_ref[...]
+    io(1).wait()
+    io(2).wait()
+    io(3).start()
 
     def project(i, carry):
-        proj = jnp.dot(attn_ref[...], tall(i), preferred_element_type=F32).astype(BF16)
-        ubuf[:, cols(i)] = (h_ref[:, cols(i)].astype(F32) + proj.astype(F32)).astype(BF16)
+        proj = jnp.dot(bbuf[...], tall(i), preferred_element_type=F32).astype(BF16)
+        ubuf[:, cols(i)] = (hbuf[:, cols(i)].astype(F32) + proj.astype(F32)).astype(BF16)
         fetch(i + RING, ('ga',))
         return carry
 
@@ -328,59 +355,84 @@
     meta(5).start()
     meta(2).wait_recv()
     ag(0, 4).wait_recv()
-    place(0, 0)
+    locate(0, 0)
+    take(0, 0, local_n)
     ag_relay(0)
     meta(3).wait_recv()
     meta(6).start()
     for k in (4, 5, 6):
         meta(k).wait_recv()
+    for o in range(1, n_pair):
+        locate(0, o)
     ag_share(0)
     ag(0, 7).wait_recv()
-    place(0, 1)
+    take(1, 0, local_n)
     ag(0, 8).wait_recv()
-    place(0, 2)
+    take(2, 0, local_n)
+    for k in range(9):
+        ag(0, k).wait_send()
+    signal_peers(x_free.at[0])
     ag_share_far(0)
+    pl.semaphore_wait(x_free.at[0], len(peers))
+    ag_own(1)
+    xbuf[0, 0] = ubuf[...]
     ag(0, 9).wait_recv()
     ag(0, 10).wait_recv()
-    place(0, 3)
-    for k in range(11):
+    take(3, 0, local_n)
+    for k in (9, 10):
         ag(0, k).wait_send()
     for k in range(7):
         meta(k).wait_send()
-    signal_peers(x_free)
-
-    def send_b():
-        pl.semaphore_wait(x_free, len(peers))
-        ag_own(1)
-        xbuf[0, 0] = ubuf[...]
+    signal_peers(x_free.at[1])
+
+    def relay_b():
+        pl.semaphore_wait(x_free.at[1], len(peers))
+        ag_relay(1)
 
     def during_a(i):
-        for when, event in ((1, send_b), (8, lambda: ag_relay(1)), (13, lambda: ag_share(1)), (18, lambda: ag_share_far(1))):
+        for when, event in ((6, relay_b), (11, lambda: ag_share(1)), (16, lambda: ag_share_far(1))):
             @pl.when(i == when)
             def _():
                 event()
 
-    gate_up(at_ga, ('ga', 'da'), during_a)
-    down(0, at_da, ('da', 'gb'))
+        @pl.when((i >= 7) & (i < 7 + n_pair))
+        def _():
+            weigh(0, i - 7)
+
+    alone = (local_n - SHARED) * n_f
+    gate_up(at_ga, 0, alone, ('ga',), during_a)
     for k in (4, 7, 8, 9, 10):
         ag(1, k).wait_recv()
     for o in range(n_pair):
-        place(1, o)
+        locate(1, o)
+        take(o, local_n - SHARED, local_n)
+    gate_up(at_ga, alone, n_ga, ('ga', 'da'), lambda i: None, both=True)
+    down(0, at_da, ('da', 'gb'))
+    for o in range(n_pair):
+        take(o, 0, local_n - SHARED)
         if o == 1:
             stage1(n_q - 1)
+    for k in range(SHARED):
+        hidden[local_n - SHARED + k] = later[k]
+    for q in (n_q - 2, n_q - 1):
+        rs(0, q).wait_send()
 
     def during_b(i):
         @pl.when((i % 2 == 1) & (i < 2 * n_q))
         def _():
             stage2(i // 2)
 
-    gate_up(at_gb, ('gb', 'db'), during_b)
-    finish(0)
-    signal_peers(rs_free)
+        @pl.when((i >= 2 * n_q) & (i < 2 * n_q + n_pair))
+        def _():
+            weigh(1, i - 2 * n_q)
+
+    io(3).wait()
+    gate_up(at_gb, 0, n_gb, ('gb', 'db'), during_b)
     down(1, at_db, ('db', 'w'))
+    io(4).start()
 
     def qkv(i, carry):
-        qkv_ref[:, cols(i)] = jnp.dot(h_ref[...], tall(at_w + i), preferred_element_type=F32).astype(BF16)
+        qbuf[:, cols(i)] = jnp.dot(hbuf[...], tall(at_w + i), preferred_element_type=F32).astype(BF16)
 
         @pl.when(i == 1)
         def _():
@@ -392,10 +444,21 @@
         return carry
 
     lax.fori_loop(0, n_w, qkv, 0)
+    io(6).start()
     stage2(n_q - 1)
-    finish(1)
+
+    def last(q, carry):
+        finish(1, q)
+        return carry
+
+    lax.fori_loop(0, n_q, last, 0)
+    io(5).start()
+    for q in (n_q - 2, n_q - 1):
+        rs(0, q).wait_send()
     for k in range(11):
         ag(1, k).wait_send()
+    for k in (4, 5, 6):
+        io(k).wait()
 
 
 def write_kernel(a_ref, b_ref, c_ref, oa_ref, ob_ref, oc_ref, va, vb, vc, sem_in, sem_out):
@@ -447,16 +510,21 @@
                 jax.ShapeDtypeStruct((tok_n, dim), BF16),
                 jax.ShapeDtypeStruct((tok_n, qkv_n), BF16),
             ),
-            in_specs=[vmem] * 7 + [hbm] * 5,
-            out_specs=(vmem, vmem, vmem),
+            in_specs=[vmem] * 4 + [hbm] * 8,
+            out_specs=(hbm, hbm, hbm),
             scratch_shapes=[
                 pltpu.VMEM((RING, dim, WIDE), BF16),
                 pltpu.VMEM((n_pair, 2, tok_n, dim), BF16),
                 pltpu.VMEM((n_pair, 2, 32, tok_n), F32),
                 pltpu.VMEM((tok_n, dim), BF16),
+                pltpu.VMEM((tok_n, dim), BF16),
+                pltpu.VMEM((tok_n, dim), BF16),
+                pltpu.VMEM((tok_n, dim), BF16),
+                pltpu.VMEM((tok_n, qkv_n), BF16),
                 pltpu.VMEM((local_n, m, dim), BF16),
                 pltpu.VMEM((local_n, m, ff), BF16),
-                pltpu.VMEM((local_n, 2 * tok_n), F32),
+                pltpu.VMEM((SHARED, m, ff), BF16),
+                pltpu.VMEM((n_pair, local_n, 2 * tok_n), F32),
                 pltpu.VMEM((n_pair, 2, 3, tok_n, local_n * cap), BF16),
                 pltpu.VMEM((n_pair, 2, local_n * cap, WIDE), BF16),
                 pltpu.VMEM((n_q, n_pair, tok_n, WIDE), F32),
@@ -466,18 +534,19 @@
                 pltpu.VMEM((n_q, tok_n, WIDE), F32),
                 pltpu.VMEM((n_q, tok_n, WIDE), F32),
                 pltpu.SemaphoreType.DMA((RING,)),
+                pltpu.SemaphoreType.DMA((7,)),
                 pltpu.SemaphoreType.DMA((2, 11)),
                 pltpu.SemaphoreType.DMA((2, 11)),
                 pltpu.SemaphoreType.DMA((7,)),
                 pltpu.SemaphoreType.DMA((7,)),
                 pltpu.SemaphoreType.DMA((n_q, 7)),
                 pltpu.SemaphoreType.DMA((n_q, 7)),
-                pltpu.SemaphoreType.REGULAR,
-                pltpu.SemaphoreType.REGULAR,
+                pltpu.SemaphoreType.REGULAR((2,)),
+                pltpu.SemaphoreType.REGULAR((n_q,)),
             ],
             compiler_params=pltpu.CompilerParams(collective_id=0, has_side_effects=True, vmem_limit_bytes=67043328),
             cost_estimate=pl.CostEstimate(flops=flops, bytes_accessed=weight_bytes, transcendentals=0),
-        )(x_a, h_b, attn_b, route_a.T, gate_a.T, route_b.T, gate_b.T, w_qkv, w_o, w_gate, w_up, w_down)
+        )(route_a.T, gate_a.T, route_b.T, gate_b.T, x_a, h_b, attn_b, w_qkv, w_o, w_gate, w_up, w_down)
         return write_out(results)
 
     row_spec = P(('dp', 'ep'), None)

time: 188 us -> 185 us (0.984)
  Pallas kernels: 187 us -> 184 us
    pallas_call x1, Pallas kernels: 184 us -> 181 us  [local_step(): pl.pallas_call(functools.partial(moe_kernel, n_devs, top_k, cap), out_sha...]
where the time goes in v4:
time: 185 us
  Pallas kernels  184 us (99%)
    pallas_call x1, Pallas kernels, local_step(): pl.pallas_call(functools.partial(moe_kernel, n_devs, top_k, cap), out_sha...  181 us

profile of v4, /device:TPU:113, one launch (start us, length us, event | category | flops | bytes accessed | tf_op | source)
XLA Modules:
  0.0 184.6 jit_solution(14714083293645699357)
XLA Ops:
  0.6 181.2 %shard_map.139 = (bf16[128,2560]{1,0:T(8,128)(2,1)}, bf16[128,2560]{1,0:T(8,128)(2,1)}, bf16[128,3584]{1,0:T(8,128)(2,1)}) custom-call(s32[6,128]{1,0:T(8,128)} %bitcast.4, f32[6,128]{1,0:T(8,128)} %bitcast.5, s32[6,128]{1,0:T(8,128)} %bitcast.6, f32[6,128]{1,0:T(8,128)} %bitcast.7, bf16[128,2560]{1,0:T(8,128)(2,1)} %x_ref.1, bf16[128,2560]{1,0:T(8,128)(2,1)} %h_ref.1, ...), custom_call_target="tpu_custom_call" | custom-call | flops 72477573120 | bytes 377487360 | tf_op jit(solution)/shard_map/pallas_call | solution.py:506
  181.8 2.6 %shard_map.140 = (bf16[128,2560]{1,0:T(8,128)(2,1)}, bf16[128,2560]{1,0:T(8,128)(2,1)}, bf16[128,3584]{1,0:T(8,128)(2,1)}) custom-call(bf16[128,2560]{1,0:T(8,128)(2,1)} %get-tuple-element.6.a_ref, bf16[128,2560]{1,0:T(8,128)(2,1)} %get-tuple-element.7.b_ref, bf16[128,3584]{1,0:T(8,128)(2,1)} %get-tuple-element.8.c_ref), custom_call_target="tpu_custom_call" | custom-call | tf_op jit(solution)/shard_map/pallas_call | solution.py:477

commit v5 on v4

--- a/solution.py
+++ b/solution.py
@@ -17,7 +17,7 @@
 def moe_kernel(n_devs, top_k, cap, ra_ref, ga_ref, rb_ref, gb_ref, x_ref, h_ref, attn_ref,
                wqkv_ref, wo_ref, wg_ref, wu_ref, wd_ref,
                outa_ref, outb_ref, qkv_ref,
-               ring, xbuf, mbuf, ubuf, abuf, bbuf, hbuf, qbuf, rows, hidden, later, slots, gts, ys, p0, p1, dr, ri, fl, fr,
+               ring, xbuf, near, mbuf, ubuf, abuf, bbuf, hbuf, qbuf, rows, hidden, later, slots, gts, ys, p0, p1, dr, ri, fl, fr,
                ring_sem, io_sem, ag_send, ag_recv, me_send, me_recv, rs_send, rs_recv, x_free, rs_free):
     tok_n, dim = x_ref.shape
     half = tok_n // 2
@@ -98,17 +98,17 @@
     lo, hi = pl.ds(0, half), pl.ds(half, half)
 
     def ag(m, k):
-        own = xbuf.at[0, 0] if m == 0 else ubuf
+        own, from_left, from_right = (xbuf.at[0, 0], xbuf.at[1, 0], xbuf.at[2, 0]) if m == 0 else (ubuf, near.at[0], near.at[1])
         src, dst, to = (
-            (own.at[lo], xbuf.at[1, 0, lo], right),
-            (own.at[hi], xbuf.at[1, 0, hi], right),
-            (own.at[hi], xbuf.at[2, 0, hi], left),
-            (own.at[lo], xbuf.at[2, 0, lo], left),
+            (own.at[lo], from_left.at[lo], right),
+            (own.at[hi], from_left.at[hi], right),
+            (own.at[hi], from_right.at[hi], left),
+            (own.at[lo], from_right.at[lo], left),
             (own, xbuf.at[0, 1], partner),
-            (xbuf.at[1, 0, lo], xbuf.at[3, 0, lo], right),
-            (xbuf.at[2, 0, hi], xbuf.at[3, 0, hi], left),
-            (xbuf.at[1, 0], xbuf.at[1, 1], partner),
-            (xbuf.at[2, 0], xbuf.at[2, 1], partner),
+            (from_left.at[lo], xbuf.at[3, 0, lo], right),
+            (from_right.at[hi], xbuf.at[3, 0, hi], left),
+            (from_left, xbuf.at[1, 1], partner),
+            (from_right, xbuf.at[2, 1], partner),
             (xbuf.at[3, 0, lo], xbuf.at[3, 1, lo], partner),
             (xbuf.at[3, 0, hi], xbuf.at[3, 1, hi], partner),
         )[k]
@@ -142,7 +142,7 @@
                                             device_id={'ep': to}, device_id_type=pl.DeviceIdType.MESH)
 
     def ag_own(m):
-        for k in range(5):
+        for k in range(4):
             ag(m, k).start()
 
     def ag_relay(m):
@@ -337,6 +337,7 @@
     for k in (0, 1, 2):
         meta(k).start()
     ag_own(0)
+    ag(0, 4).start()
     io(1).wait()
     io(2).wait()
     io(3).start()
@@ -358,6 +359,7 @@
     locate(0, 0)
     take(0, 0, local_n)
     ag_relay(0)
+    ag_own(1)
     meta(3).wait_recv()
     meta(6).start()
     for k in (4, 5, 6):
@@ -369,24 +371,20 @@
     take(1, 0, local_n)
     ag(0, 8).wait_recv()
     take(2, 0, local_n)
-    for k in range(9):
-        ag(0, k).wait_send()
-    signal_peers(x_free.at[0])
     ag_share_far(0)
-    pl.semaphore_wait(x_free.at[0], len(peers))
-    ag_own(1)
-    xbuf[0, 0] = ubuf[...]
     ag(0, 9).wait_recv()
     ag(0, 10).wait_recv()
     take(3, 0, local_n)
-    for k in (9, 10):
+    for k in range(11):
         ag(0, k).wait_send()
     for k in range(7):
         meta(k).wait_send()
-    signal_peers(x_free.at[1])
+    signal_peers(x_free)
+    xbuf[0, 0] = ubuf[...]
 
     def relay_b():
-        pl.semaphore_wait(x_free.at[1], len(peers))
+        pl.semaphore_wait(x_free, len(peers))
+        ag(1, 4).start()
         ag_relay(1)
 
     def during_a(i):
@@ -404,6 +402,8 @@
     for k in (4, 7, 8, 9, 10):
         ag(1, k).wait_recv()
     for o in range(n_pair):
+        if o in (1, 2):
+            xbuf[o, 0] = near[o - 1]
         locate(1, o)
         take(o, local_n - SHARED, local_n)
     gate_up(at_ga, alone, n_ga, ('ga', 'da'), lambda i: None, both=True)
@@ -418,13 +418,13 @@
         rs(0, q).wait_send()
 
     def during_b(i):
-        @pl.when((i % 2 == 1) & (i < 2 * n_q))
-        def _():
-            stage2(i // 2)
-
-        @pl.when((i >= 2 * n_q) & (i < 2 * n_q + n_pair))
-        def _():
-            weigh(1, i - 2 * n_q)
+        @pl.when((i % 3 == 2) & (i < 3 * n_q))
+        def _():
+            stage2(i // 3)
+
+        @pl.when((i >= 12) & (i < 12 + n_pair))
+        def _():
+            weigh(1, i - 12)
 
     io(3).wait()
     gate_up(at_gb, 0, n_gb, ('gb', 'db'), during_b)
@@ -515,6 +515,7 @@
             scratch_shapes=[
                 pltpu.VMEM((RING, dim, WIDE), BF16),
                 pltpu.VMEM((n_pair, 2, tok_n, dim), BF16),
+                pltpu.VMEM((2, tok_n, dim), BF16),
                 pltpu.VMEM((n_pair, 2, 32, tok_n), F32),
                 pltpu.VMEM((tok_n, dim), BF16),
                 pltpu.VMEM((tok_n, dim), BF16),
@@ -541,7 +542,7 @@
                 pltpu.SemaphoreType.DMA((7,)),
                 pltpu.SemaphoreType.DMA((n_q, 7)),
                 pltpu.SemaphoreType.DMA((n_q, 7)),
-                pltpu.SemaphoreType.REGULAR((2,)),
+                pltpu.SemaphoreType.REGULAR,
                 pltpu.SemaphoreType.REGULAR((n_q,)),
             ],
             compiler_params=pltpu.CompilerParams(collective_id=0, has_side_effects=True, vmem_limit_bytes=67043328),

time: 185 us -> 186 us (level)
  no operation moved by 1% of the time
where the time goes in v5:
time: 186 us; the launch traced here: 185 us
  Pallas kernels  185 us (99%)
    pallas_call x1, Pallas kernels, local_step(): pl.pallas_call(functools.partial(moe_kernel, n_devs, top_k, cap), out_sha...  182 us

profile of v5, /device:TPU:113, one launch (start us, length us, event | category | flops | bytes accessed | tf_op | source)
XLA Modules:
  0.0 185.4 jit_solution(13303155741651372887)
XLA Ops:
  0.6 182.0 %shard_map.139 = (bf16[128,2560]{1,0:T(8,128)(2,1)}, bf16[128,2560]{1,0:T(8,128)(2,1)}, bf16[128,3584]{1,0:T(8,128)(2,1)}) custom-call(s32[6,128]{1,0:T(8,128)} %bitcast.4, f32[6,128]{1,0:T(8,128)} %bitcast.5, s32[6,128]{1,0:T(8,128)} %bitcast.6, f32[6,128]{1,0:T(8,128)} %bitcast.7, bf16[128,2560]{1,0:T(8,128)(2,1)} %x_ref.1, bf16[128,2560]{1,0:T(8,128)(2,1)} %h_ref.1, ...), custom_call_target="tpu_custom_call" | custom-call | flops 72477573120 | bytes 377487360 | tf_op jit(solution)/shard_map/pallas_call | solution.py:506
  182.7 2.6 %shard_map.140 = (bf16[128,2560]{1,0:T(8,128)(2,1)}, bf16[128,2560]{1,0:T(8,128)(2,1)}, bf16[128,3584]{1,0:T(8,128)(2,1)}) custom-call(bf16[128,2560]{1,0:T(8,128)(2,1)} %get-tuple-element.6.a_ref, bf16[128,2560]{1,0:T(8,128)(2,1)} %get-tuple-element.7.b_ref, bf16[128,3584]{1,0:T(8,128)(2,1)} %get-tuple-element.8.c_ref), custom_call_target="tpu_custom_call" | custom-call | tf_op jit(solution)/shard_map/pallas_call | solution.py:477

commit v6 on v5

--- a/solution.py
+++ b/solution.py
@@ -11,13 +11,13 @@
 BF16 = jnp.bfloat16
 RING = 8
 WIDE = 512
-SHARED = 2
+SHARED = 1
 
 
 def moe_kernel(n_devs, top_k, cap, ra_ref, ga_ref, rb_ref, gb_ref, x_ref, h_ref, attn_ref,
                wqkv_ref, wo_ref, wg_ref, wu_ref, wd_ref,
                outa_ref, outb_ref, qkv_ref,
-               ring, xbuf, near, mbuf, ubuf, abuf, bbuf, hbuf, qbuf, rows, hidden, later, slots, gts, ys, p0, p1, dr, ri, fl, fr,
+               ring, xbuf, near, mbuf, ubuf, abuf, bbuf, hbuf, rows, hidden, later, slots, gts, ys, p0, p1, dr, ri, fl, fr,
                ring_sem, io_sem, ag_send, ag_recv, me_send, me_recv, rs_send, rs_recv, x_free, rs_free):
     tok_n, dim = x_ref.shape
     half = tok_n // 2
@@ -130,13 +130,14 @@
 
     def rs(k, q):
         src, dst, to = (
-            (p1.at[lax.rem(q, 2)], dr.at[q], partner),
+            (p1.at[lax.rem(q, 2), 3], dr.at[q, 3], partner),
             (p0.at[q, 3, lo], ri.at[q, 0], right),
             (p0.at[q, 3, hi], ri.at[q, 1], left),
             (p0.at[q, 2, hi], fl.at[q, hi], right),
             (p0.at[q, 1, lo], fr.at[q, lo], left),
             (p0.at[q, 2, lo], fl.at[q, lo], right),
             (p0.at[q, 1, hi], fr.at[q, hi], left),
+            (p1.at[lax.rem(q, 2), pl.ds(0, 3)], dr.at[q, pl.ds(0, 3)], partner),
         )[k]
         return pltpu.make_async_remote_copy(src_ref=src, dst_ref=dst, send_sem=rs_send.at[q, k], recv_sem=rs_recv.at[q, k],
                                             device_id={'ep': to}, device_id_type=pl.DeviceIdType.MESH)
@@ -208,7 +209,7 @@
             here = over(jnp.where(member > 0.5, slot - float(j * cap), -1.0)) == pos
             for part in range(3):
                 head = rest.astype(BF16).astype(F32)
-                gts[o, j, part] = jnp.where(here, over(head), 0.0).astype(BF16)
+                gts[o, j, part * tok_n:(part + 1) * tok_n, :] = jnp.where(here, over(head), 0.0).astype(BF16)
                 rest = rest - head
 
     def gate_up(base, begin, end, kinds, events, both=False):
@@ -233,11 +234,19 @@
 
         lax.fori_loop(begin, end, step, 0)
 
+    def far_add(q):
+        rs(0, q).wait_recv()
+        p0[q, 3] = p0[q, 3] + dr[q, 3]
+
+    def far_send(q):
+        for k in (1, 2):
+            rs(k, q).start()
+
     def stage1(q):
-        rs(0, q).wait_recv()
-        for o in (3, 2, 1, 0):
+        rs(7, q).wait_recv()
+        for o in (2, 1, 0):
             p0[q, o] = p0[q, o] + dr[q, o]
-        for k in (1, 2, 3, 4):
+        for k in (3, 4):
             rs(k, q).start()
 
     def stage2(q):
@@ -248,17 +257,19 @@
         rs(5, q).start()
         rs(6, q).start()
 
-    def combine(q):
-        for o in range(n_pair):
+    def combine(q, ready):
+        for o in (3, 2, 1, 0):
             for j in (1, 0):
-                total = None
-                for part in range(3):
-                    term = jnp.dot(gts[o, j, part], ys[o, j], preferred_element_type=F32)
-                    total = term if total is None else total + term
+                parts = jnp.dot(gts[o, j], ys[o, j], preferred_element_type=F32)
+                total = parts[:tok_n] + parts[tok_n:2 * tok_n] + parts[2 * tok_n:]
                 if j == 1:
                     p1[lax.rem(q, 2), o] = total
                 else:
                     p0[q, o] = total
+            if o == 3:
+                ready()
+                rs(0, q).start()
+        rs(7, q).start()
 
     def down(m, base, kinds):
         n_e = local_n // 2
@@ -275,8 +286,18 @@
                     here = slice(o * cap2 + j * cap, o * cap2 + (j + 1) * cap)
                     two = jnp.concatenate([y0[here], y1[here]], axis=0)
                     ys[o, j, pl.ds(pl.multiple_of(e * cap2, 16), cap2), :] = two.astype(BF16)
+            far = (e == 0) & (q >= 1)
+
+            @pl.when(far)
+            def _():
+                far_add(q - 1)
+
             fetch(at + RING, kinds)
             fetch(at + 1 + RING, kinds)
+
+            @pl.when(far)
+            def _():
+                far_send(q - 1)
 
             if m == 1:
                 @pl.when(e == 0)
@@ -294,10 +315,13 @@
                 @pl.when(q >= 2)
                 def _():
                     rs(0, q - 2).wait_send()
-                combine(q)
-                if m == 1:
-                    pl.semaphore_wait(rs_free.at[q], len(peers))
-                rs(0, q).start()
+                    rs(7, q - 2).wait_send()
+
+                def ready():
+                    if m == 1:
+                        pl.semaphore_wait(rs_free.at[q], len(peers))
+
+                combine(q, ready)
             return carry
 
         lax.fori_loop(0, n_d // 2, step, 0)
@@ -319,7 +343,8 @@
             (x_ref, abuf),
             (abuf, outa_ref),
             (bbuf, outb_ref),
-            (qbuf, qkv_ref),
+            (xbuf.at[0, 0], qkv_ref.at[:, pl.ds(0, dim)]),
+            (xbuf.at[1, 0, :, pl.ds(0, qkv_n - dim)], qkv_ref.at[:, pl.ds(dim, qkv_n - dim)]),
         )[k]
         return pltpu.make_async_copy(src, dst, io_sem.at[k])
 
@@ -398,7 +423,7 @@
             weigh(0, i - 7)
 
     alone = (local_n - SHARED) * n_f
-    gate_up(at_ga, 0, alone, ('ga',), during_a)
+    gate_up(at_ga, 0, alone, ('ga', 'da'), during_a)
     for k in (4, 7, 8, 9, 10):
         ag(1, k).wait_recv()
     for o in range(n_pair):
@@ -410,12 +435,16 @@
     down(0, at_da, ('da', 'gb'))
     for o in range(n_pair):
         take(o, 0, local_n - SHARED)
+        if o == 0:
+            far_add(n_q - 1)
         if o == 1:
+            far_send(n_q - 1)
             stage1(n_q - 1)
     for k in range(SHARED):
         hidden[local_n - SHARED + k] = later[k]
     for q in (n_q - 2, n_q - 1):
         rs(0, q).wait_send()
+        rs(7, q).wait_send()
 
     def during_b(i):
         @pl.when((i % 3 == 2) & (i < 3 * n_q))
@@ -432,10 +461,15 @@
     io(4).start()
 
     def qkv(i, carry):
-        qbuf[:, cols(i)] = jnp.dot(hbuf[...], tall(at_w + i), preferred_element_type=F32).astype(BF16)
+        xbuf[i // n_o, 0, :, cols(i % n_o)] = jnp.dot(hbuf[...], tall(at_w + i), preferred_element_type=F32).astype(BF16)
+
+        @pl.when(i == 0)
+        def _():
+            far_add(n_q - 1)
 
         @pl.when(i == 1)
         def _():
+            far_send(n_q - 1)
             stage1(n_q - 1)
 
         @pl.when((i >= 2) & (i - 2 < n_q - 1))
@@ -445,6 +479,7 @@
 
     lax.fori_loop(0, n_w, qkv, 0)
     io(6).start()
+    io(7).start()
     stage2(n_q - 1)
 
     def last(q, carry):
@@ -455,9 +490,10 @@
     io(5).start()
     for q in (n_q - 2, n_q - 1):
         rs(0, q).wait_send()
+        rs(7, q).wait_send()
     for k in range(11):
         ag(1, k).wait_send()
-    for k in (4, 5, 6):
+    for k in (4, 5, 6, 7):
         io(k).wait()
 
 
@@ -521,12 +557,11 @@
                 pltpu.VMEM((tok_n, dim), BF16),
                 pltpu.VMEM((tok_n, dim), BF16),
                 pltpu.VMEM((tok_n, dim), BF16),
-                pltpu.VMEM((tok_n, qkv_n), BF16),
                 pltpu.VMEM((local_n, m, dim), BF16),
                 pltpu.VMEM((local_n, m, ff), BF16),
                 pltpu.VMEM((SHARED, m, ff), BF16),
                 pltpu.VMEM((n_pair, local_n, 2 * tok_n), F32),
-                pltpu.VMEM((n_pair, 2, 3, tok_n, local_n * cap), BF16),
+                pltpu.VMEM((n_pair, 2, 3 * tok_n, local_n * cap), BF16),
                 pltpu.VMEM((n_pair, 2, local_n * cap, WIDE), BF16),
                 pltpu.VMEM((n_q, n_pair, tok_n, WIDE), F32),
                 pltpu.VMEM((2, n_pair, tok_n, WIDE), F32),
@@ -535,13 +570,13 @@
                 pltpu.VMEM((n_q, tok_n, WIDE), F32),
                 pltpu.VMEM((n_q, tok_n, WIDE), F32),
                 pltpu.SemaphoreType.DMA((RING,)),
-                pltpu.SemaphoreType.DMA((7,)),
+                pltpu.SemaphoreType.DMA((8,)),
                 pltpu.SemaphoreType.DMA((2, 11)),
                 pltpu.SemaphoreType.DMA((2, 11)),
                 pltpu.SemaphoreType.DMA((7,)),
                 pltpu.SemaphoreType.DMA((7,)),
-                pltpu.SemaphoreType.DMA((n_q, 7)),
-                pltpu.SemaphoreType.DMA((n_q, 7)),
+                pltpu.SemaphoreType.DMA((n_q, 8)),
+                pltpu.SemaphoreType.DMA((n_q, 8)),
                 pltpu.SemaphoreType.REGULAR,
                 pltpu.SemaphoreType.REGULAR((n_q,)),
             ],

time: 186 us -> 186 us (level)
  no operation moved by 1% of the time
where the time goes in v6:
time: 186 us
  Pallas kernels  185 us (99%)
    pallas_call x1, Pallas kernels, local_step(): pl.pallas_call(functools.partial(moe_kernel, n_devs, top_k, cap), out_sha...  182 us

profile of v6, /device:TPU:113, one launch (start us, length us, event | category | flops | bytes accessed | tf_op | source)
XLA Modules:
  0.0 185.6 jit_solution(11246512524027098664)
XLA Ops:
  0.6 182.2 %shard_map.139 = (bf16[128,2560]{1,0:T(8,128)(2,1)}, bf16[128,2560]{1,0:T(8,128)(2,1)}, bf16[128,3584]{1,0:T(8,128)(2,1)}) custom-call(s32[6,128]{1,0:T(8,128)} %bitcast.4, f32[6,128]{1,0:T(8,128)} %bitcast.5, s32[6,128]{1,0:T(8,128)} %bitcast.6, f32[6,128]{1,0:T(8,128)} %bitcast.7, bf16[128,2560]{1,0:T(8,128)(2,1)} %x_ref.1, bf16[128,2560]{1,0:T(8,128)(2,1)} %h_ref.1, ...), custom_call_target="tpu_custom_call" | custom-call | flops 72477573120 | bytes 377487360 | tf_op jit(solution)/shard_map/pallas_call | solution.py:542
  182.9 2.6 %shard_map.140 = (bf16[128,2560]{1,0:T(8,128)(2,1)}, bf16[128,2560]{1,0:T(8,128)(2,1)}, bf16[128,3584]{1,0:T(8,128)(2,1)}) custom-call(bf16[128,2560]{1,0:T(8,128)(2,1)} %get-tuple-element.6.a_ref, bf16[128,2560]{1,0:T(8,128)(2,1)} %get-tuple-element.7.b_ref, bf16[128,3584]{1,0:T(8,128)(2,1)} %get-tuple-element.8.c_ref), custom_call_target="tpu_custom_call" | custom-call | tf_op jit(solution)/shard_map/pallas_call | solution.py:513

commit v7 on v6

--- a/solution.py
+++ b/solution.py
@@ -11,7 +11,7 @@
 BF16 = jnp.bfloat16
 RING = 8
 WIDE = 512
-SHARED = 1
+SHARED = 2
 
 
 def moe_kernel(n_devs, top_k, cap, ra_ref, ga_ref, rb_ref, gb_ref, x_ref, h_ref, attn_ref,
@@ -447,9 +447,9 @@
         rs(7, q).wait_send()
 
     def during_b(i):
-        @pl.when((i % 3 == 2) & (i < 3 * n_q))
-        def _():
-            stage2(i // 3)
+        @pl.when((i % 2 == 1) & (i < 2 * n_q))
+        def _():
+            stage2(i // 2)
 
         @pl.when((i >= 12) & (i < 12 + n_pair))
         def _():

time: 186 us -> 184 us (0.989)
  Pallas kernels: 185 us -> 183 us
    pallas_call x1, Pallas kernels: 182 us -> 180 us  [local_step(): pl.pallas_call(functools.partial(moe_kernel, n_devs, top_k, cap), out_sha...]
where the time goes in v7:
time: 184 us
  Pallas kernels  183 us (99%)
    pallas_call x1, Pallas kernels, local_step(): pl.pallas_call(functools.partial(moe_kernel, n_devs, top_k, cap), out_sha...  180 us

profile of v7, /device:TPU:113, one launch (start us, length us, event | category | flops | bytes accessed | tf_op | source)
XLA Modules:
  0.0 183.7 jit_solution(6067437245203811597)
XLA Ops:
  0.6 180.4 %shard_map.139 = (bf16[128,2560]{1,0:T(8,128)(2,1)}, bf16[128,2560]{1,0:T(8,128)(2,1)}, bf16[128,3584]{1,0:T(8,128)(2,1)}) custom-call(s32[6,128]{1,0:T(8,128)} %bitcast.4, f32[6,128]{1,0:T(8,128)} %bitcast.5, s32[6,128]{1,0:T(8,128)} %bitcast.6, f32[6,128]{1,0:T(8,128)} %bitcast.7, bf16[128,2560]{1,0:T(8,128)(2,1)} %x_ref.1, bf16[128,2560]{1,0:T(8,128)(2,1)} %h_ref.1, ...), custom_call_target="tpu_custom_call" | custom-call | flops 72477573120 | bytes 377487360 | tf_op jit(solution)/shard_map/pallas_call | solution.py:542
  181.0 2.6 %shard_map.140 = (bf16[128,2560]{1,0:T(8,128)(2,1)}, bf16[128,2560]{1,0:T(8,128)(2,1)}, bf16[128,3584]{1,0:T(8,128)(2,1)}) custom-call(bf16[128,2560]{1,0:T(8,128)(2,1)} %get-tuple-element.6.a_ref, bf16[128,2560]{1,0:T(8,128)(2,1)} %get-tuple-element.7.b_ref, bf16[128,3584]{1,0:T(8,128)(2,1)} %get-tuple-element.8.c_ref), custom_call_target="tpu_custom_call" | custom-call | tf_op jit(solution)/shard_map/pallas_call | solution.py:513
